TPU v7x, 32 devices: a whole 2x2x4 slice. The times are simulated.
32 devices in a mesh: cp: 8 (over z, y), fsdp: 4 (over x, core).
Axes of the slice: x: 2, y: 2, z: 4, core: 2. Of those that a mesh axis runs over, the one named last changes fastest.
Arguments:
- query_states: bfloat16 [4, 1024, 1024], P('fsdp', 'cp'), may hold values from -32 to 32
- key_states: bfloat16 [4, 1024, 1024], P('fsdp', 'cp'), may hold values from -32 to 32
- value_states: bfloat16 [4, 1024, 1024], P('fsdp', 'cp'), may hold values from -6 to 6
- span_order: int32 [16], replicated, may hold values from 0 to 15, as said below
- block_mask: int32 [16, 16], replicated, may hold values from 0 to 1, as said below
- output_weight: bfloat16 [1024, 2048], P(('cp', 'fsdp')), may hold values from -0.1875 to 0.1875
- upstream: bfloat16 [4, 1024, 2048], P('fsdp', 'cp'), may hold values from -6 to 6
Outputs:
- projected: bfloat16 [4, 1024, 2048], P('fsdp', 'cp')
- query_gradient: bfloat16 [4, 1024, 1024], P('fsdp', 'cp')
- key_gradient: bfloat16 [4, 1024, 1024], P('fsdp', 'cp')
- value_gradient: bfloat16 [4, 1024, 1024], P('fsdp', 'cp')
- weight_gradient: float32 [1024, 2048], P(('cp', 'fsdp'))
Inputs may be any that keep to these rules, and one draw needn't show every extreme that they name: `span_order`: entries 2 d and 2 d + 1 hold positions p and 15 - p; every position appears once. `block_mask`: the diagonal is 1.
All inputs are finite; a program needn't handle non-finite values.
Results may differ from a plain program's by a relative error of at most 0.024.
Values may be sent and summed in bfloat16 or wider, within the bound.
A program may use at most 128 MiB of HBM per device.

v0:
```python
import math

import jax
import jax.numpy as jnp
from jax import lax
from jax.experimental import pallas as pl
from jax.experimental.pallas import tpu as pltpu
from jax.sharding import PartitionSpec as P

HEADS = 8
HEAD = 128


lowest = -1e30


def split_heads(row_block):
    return row_block.reshape(row_block.shape[0], HEADS, HEAD)


def pair_scores(query_rows, key_rows):
    return jnp.einsum(
        "qhd,khd->hqk",
        split_heads(query_rows),
        split_heads(key_rows),
        preferred_element_type=jnp.float32,
    ) * (1.0 / HEAD)


def storage_mask(span_order, block_mask):
    span_count = span_order.shape[0]
    onehot = (span_order[:, None] == jnp.arange(span_count, dtype=jnp.int32)[None, :]).astype(
        jnp.float32
    )
    permuted = jnp.dot(jnp.dot(onehot, block_mask.astype(jnp.float32)), onehot.T)
    return permuted > 0.5


def allowed_block(span_ok, positions, query_begin, query_total, key_begin, key_total, span_rows):
    span_sub = lax.dynamic_slice(
        span_ok,
        (query_begin // span_rows, key_begin // span_rows),
        (query_total // span_rows, key_total // span_rows),
    )
    spread = jnp.broadcast_to(
        span_sub[:, None, :, None],
        (query_total // span_rows, span_rows, key_total // span_rows, span_rows),
    )
    spread = spread.reshape(query_total, key_total)
    query_pos = lax.dynamic_slice_in_dim(positions, query_begin, query_total)
    key_pos = lax.dynamic_slice_in_dim(positions, key_begin, key_total)
    return spread & (key_pos[None, :] <= query_pos[:, None])


def local_terms(query_rows, grad_rows, log_rows, delta_rows, key_rows, value_rows, allowed):
    scores = pair_scores(query_rows, key_rows)
    probability = jnp.where(allowed[None], jnp.exp(scores - log_rows[..., None]), 0.0)
    dprob = jnp.einsum(
        "qhd,khd->hqk",
        split_heads(grad_rows),
        split_heads(value_rows),
        preferred_element_type=jnp.float32,
    )
    dscores = (probability * (dprob - delta_rows[..., None]) * (1.0 / HEAD)).astype(jnp.bfloat16)
    return (probability, dscores)


def local(query_states, key_states, value_states, span_order, block_mask, output_weight, upstream):
    query_rows = query_states[0]
    key_local = key_states[0]
    value_local = value_states[0]
    upstream_rows = upstream[0]
    tokens = query_rows.shape[0]
    span_rows = tokens // 2
    positions = (
        span_order[:, None] * span_rows + jnp.arange(span_rows, dtype=jnp.int32)[None, :]
    ).reshape(-1)
    span_ok = storage_mask(span_order, block_mask)
    own_start = lax.axis_index("cp") * tokens
    key_all, value_all = (
        lax.all_gather(key_local, "cp", axis=0, tiled=True),
        lax.all_gather(value_local, "cp", axis=0, tiled=True),
    )
    weight = lax.all_gather(output_weight, ("cp", "fsdp"), axis=0, tiled=True)
    length = key_all.shape[0]
    key_block = math.gcd(length, 512)
    block_count = length // key_block
    block_steps = jnp.arange(block_count, dtype=jnp.int32)

    def stats_step(running, step_index):
        key_begin = step_index * key_block
        key_rows = lax.dynamic_slice_in_dim(key_all, key_begin, key_block)
        allowed = allowed_block(
            span_ok, positions, own_start, tokens, key_begin, key_block, span_rows
        )
        maxima, totals = running
        scores = pair_scores(query_rows, key_rows)
        masked = jnp.where(allowed[None], scores, lowest)
        new_max = jnp.maximum(maxima, masked.max(-1))
        exp_terms = jnp.where(allowed[None], jnp.exp(scores - new_max[..., None]), 0.0)
        return ((new_max, totals * jnp.exp(maxima - new_max) + exp_terms.sum(-1)), None)

    stat_start = (
        jnp.full((HEADS, tokens), lowest, jnp.float32),
        jnp.zeros((HEADS, tokens), jnp.float32),
    )
    (maxima, totals), _ = lax.scan(stats_step, stat_start, block_steps)
    log_total = maxima + jnp.log(totals)

    def output_step(attn_sum, step_index):
        key_begin = step_index * key_block
        key_rows = lax.dynamic_slice_in_dim(key_all, key_begin, key_block)
        value_rows = lax.dynamic_slice_in_dim(value_all, key_begin, key_block)
        allowed = allowed_block(
            span_ok, positions, own_start, tokens, key_begin, key_block, span_rows
        )
        scores = pair_scores(query_rows, key_rows)
        probability = jnp.where(allowed[None], jnp.exp(scores - log_total[..., None]), 0.0)
        return (
            attn_sum
            + jnp.einsum(
                "hqk,khd->qhd",
                probability.astype(jnp.bfloat16),
                split_heads(value_rows),
                preferred_element_type=jnp.float32,
            ),
            None,
        )

    zero_heads = jnp.zeros((tokens, HEADS, HEAD), jnp.float32)
    attn_sum, _ = lax.scan(output_step, zero_heads, block_steps)
    attended = lax.optimization_barrier(attn_sum.reshape(tokens, -1).astype(jnp.bfloat16))
    projected = jnp.dot(attended, weight, preferred_element_type=jnp.float32).astype(jnp.bfloat16)
    grad_attended = lax.dot_general(
        upstream_rows, weight, (((1,), (1,)), ((), ())), preferred_element_type=jnp.float32
    ).astype(jnp.bfloat16)
    grad_attended = lax.optimization_barrier(grad_attended)
    weight_term = lax.dot_general(
        attended, upstream_rows, (((0,), (0,)), ((), ())), preferred_element_type=jnp.float32
    )
    row_delta = (
        (grad_attended.astype(jnp.float32) * attended.astype(jnp.float32))
        .reshape(tokens, HEADS, HEAD)
        .sum(-1)
    )
    delta_heads = row_delta.T

    def query_step(grad_sum, step_index):
        key_begin = step_index * key_block
        key_rows = lax.dynamic_slice_in_dim(key_all, key_begin, key_block)
        value_rows = lax.dynamic_slice_in_dim(value_all, key_begin, key_block)
        allowed = allowed_block(
            span_ok, positions, own_start, tokens, key_begin, key_block, span_rows
        )
        probability, dscores = local_terms(
            query_rows, grad_attended, log_total, delta_heads, key_rows, value_rows, allowed
        )
        return (
            grad_sum
            + jnp.einsum(
                "hqk,khd->qhd", dscores, split_heads(key_rows), preferred_element_type=jnp.float32
            ),
            None,
        )

    query_sum, _ = lax.scan(query_step, zero_heads, block_steps)
    query_gradient = query_sum.reshape(tokens, -1).astype(jnp.bfloat16)
    log_all, delta_all = (
        lax.all_gather(log_total.T, "cp", axis=0, tiled=True),
        lax.all_gather(row_delta, "cp", axis=0, tiled=True),
    )
    sums_now = (zero_heads, zero_heads)
    query_piece = lax.all_gather(query_rows, "cp", axis=0, tiled=True)
    grad_piece = lax.all_gather(grad_attended, "cp", axis=0, tiled=True)
    row_count = query_piece.shape[0]
    sources = row_count // tokens
    group_size = math.gcd(sources, max(1, 512 // tokens))
    group_rows = group_size * tokens

    def group_step(running, step_index):
        offset = step_index * group_rows
        query_group = lax.dynamic_slice_in_dim(query_piece, offset, group_rows)
        grad_group = lax.dynamic_slice_in_dim(grad_piece, offset, group_rows)
        log_group = lax.dynamic_slice_in_dim(log_all, offset, group_rows).T
        delta_group = lax.dynamic_slice_in_dim(delta_all, offset, group_rows).T
        allowed = allowed_block(
            span_ok, positions, offset, group_rows, own_start, tokens, span_rows
        )
        key_sum, value_sum = running
        probability, dscores = local_terms(
            query_group, grad_group, log_group, delta_group, key_local, value_local, allowed
        )
        probability_low = probability.astype(jnp.bfloat16).reshape(
            HEADS, group_size, tokens, tokens
        )
        dscores_group = dscores.reshape(HEADS, group_size, tokens, tokens)
        qsplit = query_group.reshape(group_size, tokens, HEADS, HEAD)
        gsplit = grad_group.reshape(group_size, tokens, HEADS, HEAD)
        key_part = jnp.einsum(
            "hgqk,gqhd->gkhd", dscores_group, qsplit, preferred_element_type=jnp.float32
        ).astype(jnp.bfloat16)
        value_part = jnp.einsum(
            "hgqk,gqhd->gkhd", probability_low, gsplit, preferred_element_type=jnp.float32
        ).astype(jnp.bfloat16)
        key_part, value_part = lax.optimization_barrier((key_part, value_part))
        return (
            (
                key_sum + key_part.astype(jnp.float32).sum(0),
                value_sum + value_part.astype(jnp.float32).sum(0),
            ),
            None,
        )

    sums_now, _ = lax.scan(group_step, sums_now, jnp.arange(sources // group_size, dtype=jnp.int32))
    key_sum, value_sum = sums_now
    key_gradient = key_sum.reshape(tokens, -1).astype(jnp.bfloat16)
    value_gradient = value_sum.reshape(tokens, -1).astype(jnp.bfloat16)
    cycle_count = lax.axis_size("cp")
    batch_count = lax.axis_size("fsdp")
    slab_rows = weight_term.shape[0] // (cycle_count * batch_count)
    reordered = weight_term.reshape(cycle_count, batch_count, slab_rows, -1).transpose(1, 0, 2, 3)
    reordered = reordered.reshape(weight_term.shape[0], -1)
    partial_batch = lax.psum_scatter(
        reordered.astype(jnp.bfloat16), "fsdp", scatter_dimension=0, tiled=True
    )
    weight_gradient = lax.psum_scatter(partial_batch, "cp", scatter_dimension=0, tiled=True).astype(
        jnp.float32
    )
    return (
        projected[None],
        query_gradient[None],
        key_gradient[None],
        value_gradient[None],
        weight_gradient,
    )


MESH = pl.DeviceIdType.MESH


def remote(src, dst, send_sem, recv_sem, device):
    return pltpu.make_async_remote_copy(
        src_ref=src,
        dst_ref=dst,
        send_sem=send_sem,
        recv_sem=recv_sem,
        device_id=device,
        device_id_type=MESH,
    )


def rows_of(begin, count):
    return pl.ds(pl.multiple_of(begin, count), count)


def greet(devices):
    barrier = pltpu.get_barrier_semaphore()
    for device in devices:
        pl.semaphore_signal(barrier, inc=1, device_id=device, device_id_type=MESH)
    pl.semaphore_wait(barrier, len(devices))


def layer_kernel(
    n, q, k, v, up, w, allowed, proj, dq, dk, dv, wg,
    qh, kh, vh, ups, wall, prob, att, attended, dqh, dkh, dvh, dk_sum, dv_sum, dw_sum, dw, dwr,
    kt, vt, local_sem, heads_s, heads_r, out_s, out_r, ring_s, ring_r,
    part_s, part_r, cross_s, cross_r, relay_s, relay_r, ws, wr,
):
    me = lax.axis_index("cp")
    col = lax.axis_index("fsdp")
    partner = {"fsdp": col + 1 - 2 * lax.rem(col, 2)}
    cross_col = lax.rem(col + 2, 4)
    cross = {"fsdp": cross_col}
    tokens = up.shape[0]
    half = tokens // 2
    slab = w.shape[0]
    depth = n // 2
    zed, why = me // 2, lax.rem(me, 2)
    place = zed + why * (n - 1 - 2 * zed)

    def at_place(offset):
        r = lax.rem(place + offset + 2 * n, n)
        return 2 * r + (r // depth) * (2 * n - 1 - 4 * r)

    def head_cols(d):
        return rows_of(d * HEAD, HEAD)

    peers = [{"cp": lax.rem(me + i, n)} for i in range(1, n)]
    columns = [{"fsdp": lax.rem(col + j, 4)} for j in range(1, 4)]
    greet(peers + columns)

    def chunk_ref(which, owner):
        if which == 2:
            return wall.at[rows_of(owner * (4 * slab) + col * slab, slab)]
        return ups.at[rows_of(owner * tokens + which * half, half)]

    def own_ref(which):
        if which == 2:
            return w
        return up.at[rows_of(which * half, half)]

    sends = []
    toward = ({"cp": at_place(1)}, {"cp": at_place(-1)})

    def chunks_at(step, way):
        if step < depth:
            return (2, 0, 1)
        return (2, 0) if way == 0 else (1,)

    def ring_start(step, way, which):
        owner = at_place((1 - step) if way == 0 else (step - 1))
        source = own_ref(which) if step == 1 else chunk_ref(which, owner)
        copy = remote(
            source, chunk_ref(which, owner),
            ring_s.at[way, step, which], ring_r.at[way, step, which], toward[way],
        )
        copy.start()
        sends.append(copy)

    def ring_wait(step, way, which):
        owner = at_place(-step if way == 0 else step)
        block = chunk_ref(which, owner)
        remote(
            block, block, ring_s.at[way, step, which], ring_r.at[way, step, which], toward[way]
        ).wait_recv()

    spread = []

    def spread_weight(owner, source):
        slot = len(spread)
        spread.append(owner)
        block = chunk_ref(2, owner)
        for device, ss, rs in ((cross, cross_s, cross_r), (partner, part_s, part_r)):
            copy = remote(source, block, ss.at[slot], rs.at[slot], device)
            copy.start()
            sends.append(copy)

    for way in range(2):
        for which in chunks_at(1, way):
            ring_start(1, way, which)
    triples = ((q, qh), (k, kh), (v, vh))
    for i in range(1, n):
        d = lax.rem(me + i, n)
        for t, (a, b) in enumerate(triples):
            copy = remote(
                a.at[:, head_cols(d)], b.at[rows_of(me * tokens, tokens)],
                heads_s.at[t, i], heads_r.at[t, i], {"cp": d},
            )
            copy.start()
            sends.append(copy)
    own = [
        pltpu.make_async_copy(
            a.at[:, head_cols(me)], b.at[rows_of(me * tokens, tokens)], local_sem.at[t]
        )
        for t, (a, b) in enumerate(triples)
    ]
    own.append(pltpu.make_async_copy(up, ups.at[rows_of(me * tokens, tokens)], local_sem.at[3]))
    own.append(pltpu.make_async_copy(w, chunk_ref(2, me), local_sem.at[4]))
    for copy in own:
        copy.start()
    spread_weight(me, w)
    bf16, f32 = jnp.bfloat16, jnp.float32
    nt = (((1,), (1,)), ((), ()))
    near = partner["fsdp"]
    far = lax.rem(near + 2, 4)

    def relay(slot):
        block = wall.at[rows_of(spread[slot] * (4 * slab) + cross_col * slab, slab)]
        remote(block, block, cross_s.at[slot], cross_r.at[slot], cross).wait_recv()
        copy = remote(block, block, relay_s.at[slot], relay_r.at[slot], partner)
        copy.start()
        sends.append(copy)

    def weight_wait(slot):
        for other, ss, rs in ((near, part_s, part_r), (far, relay_s, relay_r)):
            block = wall.at[rows_of(spread[slot] * (4 * slab) + other * slab, slab)]
            remote(block, block, ss.at[slot], rs.at[slot], partner).wait_recv()

    def advance(step, chunks):
        for which in chunks:
            for way in range(2):
                if which not in chunks_at(step, way):
                    continue
                ring_wait(step, way, which)
                if step < depth and which in chunks_at(step + 1, way):
                    ring_start(step + 1, way, which)
                if which == 2:
                    owner = at_place(-step if way == 0 else step)
                    spread_weight(owner, chunk_ref(2, owner))

    def out_send(t, i, source, target):
        d = lax.rem(me + i, n)
        copy = remote(
            source.at[rows_of(d * tokens, tokens)], target.at[:, head_cols(me)],
            out_s.at[t, i], out_r.at[t, i], {"cp": d},
        )
        copy.start()
        sends.append(copy)

    def out_wait(t, target):
        for i in range(1, n):
            source = lax.rem(me + n - i, n)
            block = target.at[:, head_cols(source)]
            remote(block, block, out_s.at[t, i], out_r.at[t, i], {"cp": source}).wait_recv()

    advance(1, (2, 0, 1))
    relay(0)
    for i in range(1, n):
        source = lax.rem(me + n - i, n)
        for t, (a, b) in enumerate(triples):
            block = b.at[rows_of(source * tokens, tokens)]
            remote(block, block, heads_s.at[t, i], heads_r.at[t, i], {"cp": source}).wait_recv()
    for copy in own:
        copy.wait()
    kt[...] = kh[...].astype(f32).T.astype(bf16)
    vt[...] = vh[...].astype(f32).T.astype(bf16)
    dk_sum[...] = jnp.zeros_like(dk_sum)
    dv_sum[...] = jnp.zeros_like(dv_sum)
    dw_sum[...] = jnp.zeros_like(dw_sum)

    def forward(o, carry):
        rows = rows_of(o * tokens, tokens)
        scores = lax.dot_general(kh[...], qh[rows], nt, preferred_element_type=f32) * (1.0 / HEAD)
        scores = jnp.where(allowed[:, rows].astype(f32) > 0.5, scores, lowest)
        terms = jnp.exp(scores - scores.max(0, keepdims=True))
        probability = terms * (1.0 / terms.sum(0, keepdims=True))
        prob[:, rows] = probability
        att_t = jnp.dot(vt[...], probability.astype(bf16), preferred_element_type=f32)
        att[rows] = att_t.T.astype(bf16)
        return carry

    lax.fori_loop(0, n, forward, 0)
    weight_wait(0)
    for i in range(1, n):
        out_send(0, i, att, attended)
    attended[:, head_cols(me)] = att[rows_of(me * tokens, tokens)]

    def backward(o):
        rows = rows_of(o * tokens, tokens)
        up_rows = ups[rows]
        ga = lax.dot_general(
            up_rows, wall[rows_of(me * HEAD, HEAD)], nt, preferred_element_type=f32
        ).astype(bf16)
        att_rows = att[rows]
        delta = (att_rows.astype(f32) * ga.astype(f32)).T.sum(0, keepdims=True)
        dprob = lax.dot_general(vh[...], ga, nt, preferred_element_type=f32)
        probability = prob[:, rows]
        ds = (probability * (dprob - delta) * (1.0 / HEAD)).astype(bf16)
        dqh[rows] = jnp.dot(kt[...], ds, preferred_element_type=f32).T.astype(bf16)
        dk_sum[...] += jnp.dot(ds, qh[rows], preferred_element_type=f32)
        dv_sum[...] += jnp.dot(probability.astype(bf16), ga, preferred_element_type=f32)
        dw_sum[...] += lax.dot_general(
            att_rows, up_rows, (((0,), (0,)), ((), ())), preferred_element_type=f32
        )

    def query_send(o):
        i = lax.rem(o + n - me, n)
        copy = remote(
            dqh.at[rows_of(o * tokens, tokens)], dq.at[:, head_cols(me)],
            out_s.at[3, i], out_r.at[3, i], {"cp": o},
        )
        copy.start()
        sends.append(copy)

    backward(me)
    for step in range(2, depth + 1):
        advance(step, (2, 0))
        if step > 2:
            for offset in (2 - step, step - 2):
                query_send(at_place(offset))
        relay(2 * step - 3)
        backward(at_place(1 - step))
        advance(step, (1,))
        relay(2 * step - 2)
        backward(at_place(step - 1))
    backward(at_place(depth))
    dkh[...] = dk_sum[...].astype(bf16)
    dvh[...] = dv_sum[...].astype(bf16)
    dw[...] = dw_sum[...].astype(bf16)
    triples_out = ((dkh, dk), (dvh, dv), (dqh, dq))
    mine = rows_of(me * tokens, tokens)
    for t, (a, b) in enumerate(triples_out):
        b[:, head_cols(me)] = a[mine]
        if t < 2:
            for i in range(1, n):
                out_send(t + 1, i, a, b)
    for offset in (1 - depth, depth - 1, depth):
        query_send(at_place(offset))
    for j in range(1, 4):
        g = lax.rem(col + j, 4)
        copy = remote(dw.at[rows_of(g * slab, slab)], dwr.at[j], ws.at[j], wr.at[j], {"fsdp": g})
        copy.start()
        sends.append(copy)
    relay(len(spread) - 1)
    for slot in range(1, len(spread)):
        weight_wait(slot)
    out_wait(0, attended)
    width = math.gcd(proj.shape[1], 512)

    def project(i, carry):
        cols = rows_of(i * width, width)
        proj[:, cols] = jnp.dot(
            attended[...], wall[:, cols], preferred_element_type=f32
        ).astype(bf16)
        return carry

    lax.fori_loop(0, proj.shape[1] // width, project, 0)
    for j in range(1, 4):
        block = dwr.at[j]
        remote(block, block, ws.at[j], wr.at[j], columns[j - 1]).wait_recv()
    total = dw[rows_of(col * slab, slab)].astype(f32)
    for j in range(1, 4):
        total = total + dwr[j].astype(f32)
    wg[...] = total
    for t, (a, b) in enumerate(triples_out):
        out_wait(t + 1, b)
    for copy in sends:
        copy.wait_send()


def by_heads(query_states, key_states, value_states, span_order, block_mask, output_weight, upstream):
    n = lax.axis_size("cp")
    m = lax.axis_size("fsdp")
    tokens, width = query_states.shape[1:]
    length = tokens * n
    model = upstream.shape[2]
    slab = output_weight.shape[0]
    span_rows = tokens // 2
    bf16, f32 = jnp.bfloat16, jnp.float32
    shape = jax.ShapeDtypeStruct
    vmem = pl.BlockSpec(memory_space=pltpu.VMEM)
    dma = pltpu.SemaphoreType.DMA
    half = n // 2
    positions = (
        span_order[:, None] * span_rows + jnp.arange(span_rows, dtype=jnp.int32)[None, :]
    ).reshape(-1)
    spans = span_order.shape[0]
    member = (
        jnp.arange(length, dtype=jnp.int32)[:, None] // span_rows
        == jnp.arange(spans, dtype=jnp.int32)[None, :]
    ).astype(bf16)
    span_ok = storage_mask(span_order, block_mask).astype(bf16)
    key_side = lax.dot_general(member, span_ok, (((1,), (1,)), ((), ())), preferred_element_type=bf16)
    seen = lax.dot_general(key_side, member, (((1,), (1,)), ((), ())), preferred_element_type=f32)
    allowed = ((seen > 0.5) & (positions[:, None] <= positions[None, :])).astype(bf16)
    head_array = pltpu.VMEM((length, HEAD), bf16)
    head_sum = pltpu.VMEM((length, HEAD), f32)
    projected, dq, dk, dv, weight_gradient = pl.pallas_call(
        lambda *refs: layer_kernel(n, *refs),
        out_shape=(shape((tokens, model), bf16),)
        + (shape((tokens, width), bf16),) * 3
        + (shape((slab, model), f32),),
        in_specs=[vmem] * 6,
        out_specs=(vmem,) * 5,
        scratch_shapes=[
            head_array, head_array, head_array,
            pltpu.VMEM((length, model), bf16), pltpu.VMEM((width, model), bf16),
            pltpu.VMEM((length, length), f32), head_array, pltpu.VMEM((tokens, width), bf16),
            head_array, head_array, head_array, head_sum, head_sum,
            pltpu.VMEM((HEAD, model), f32), pltpu.VMEM((HEAD, model), bf16),
            pltpu.VMEM((m, slab, model), bf16),
            pltpu.VMEM((HEAD, length), bf16), pltpu.VMEM((HEAD, length), bf16),
            dma((5,)), dma((3, n)), dma((3, n)), dma((4, n)), dma((4, n)),
            dma((2, half + 1, 3)), dma((2, half + 1, 3)),
        ]
        + [dma((n,))] * 6 + [dma((m,))] * 2,
        compiler_params=pltpu.CompilerParams(
            collective_id=0, has_side_effects=True, vmem_limit_bytes=48 << 20
        ),
        name="layer",
    )(query_states[0], key_states[0], value_states[0], upstream[0], output_weight, allowed)
    return (projected[None], dq[None], dk[None], dv[None], weight_gradient)


def solution(mesh):
    fits = mesh.shape["cp"] == HEADS and mesh.shape["fsdp"] == 4
    return jax.shard_map(
        by_heads if fits else local,
        mesh=mesh,
        in_specs=(
            P("fsdp", "cp", None),
            P("fsdp", "cp", None),
            P("fsdp", "cp", None),
            P(),
            P(),
            P(("cp", "fsdp"), None),
            P("fsdp", "cp", None),
        ),
        out_specs=(
            P("fsdp", "cp", None),
            P("fsdp", "cp", None),
            P("fsdp", "cp", None),
            P("fsdp", "cp", None),
            P(("cp", "fsdp"), None),
        ),
        check_vma=False,
    )
```

profile of v0, /device:TPU:0, one launch (start us, length us, event | category | flops | bytes accessed | tf_op | source)
XLA Modules:
  0.0 106.7 jit_solution(15024164037865930722)
XLA Ops:
  0.6 0.0 copy-start
  0.6 0.0 copy-start.4
  0.7 0.0 copy-start.3
  0.7 0.0 copy-start.2
  0.7 0.0 copy-start.1
  0.7 0.8 broadcast_multiply_fusion
  1.4 1.0 fusion.5
  2.5 0.1 iota_add_fusion
  2.6 0.1 add.33
  2.6 1.0 and_convert_fusion.refs_5_
  3.6 0.0 copy-done
  3.6 0.0 copy-done.4
  3.6 0.0 copy-done.3
  3.7 0.0 copy-done.2
  3.7 0.0 copy-done.1
  3.7 99.4 %layer.1 = (bf16[128,2048]{1,0:T(8,128)(2,1)S(1)}, bf16[128,1024]{1,0:T(8,128)(2,1)S(1)}, bf16[128,1024]{1,0:T(8,128)(2,1)S(1)}, bf16[128,1024]{1,0:T(8,128)(2,1)S(1)}, f32[32,2048]{1,0:T(8,128)S(1)}) custom-call(bf16[128,1024]{1,0:T(8,128)(2,1)S(1)} %bitcast.11, bf16[128,1024]{1,0:T(8,128)(2,1)S(1)} %bitcast.12, bf16[128,1024]{1,0:T(8,128)(2,1)S(1)} %bitcast.13, ...), custom_call_target="tpu_custom_call" | custom-call | tf_op jit(solution)/shard_map/layer/pallas_call | solution.py:548
  103.1 0.8 copy.17
  103.9 0.7 copy.18
  104.6 0.7 copy.19
  105.3 0.7 copy.20
  106.0 0.7 copy.21
  (1 shorter events, 0.0 us)
Async XLA Ops:
  0.6 3.0 %copy-start = (bf16[1,128,2048]{2,1,0:T(8,128)(2,1)S(1)}, bf16[1,128,2048]{2,1,0:T(8,128)(2,1)}, u32[]{:S(2)}) copy-start(bf16[1,128,2048]{2,1,0:T(8,128)(2,1)} %param.13) | copy-start | bytes 1572868
  0.6 3.0 %copy-start.4 = (bf16[32,2048]{1,0:T(8,128)(2,1)S(1)}, bf16[32,2048]{1,0:T(8,128)(2,1)}, u32[]{:S(2)}) copy-start(bf16[32,2048]{1,0:T(8,128)(2,1)} %refs_4_.1) | copy-start | bytes 393220
  0.7 3.0 %copy-start.3 = (bf16[1,128,1024]{2,1,0:T(8,128)(2,1)S(1)}, bf16[1,128,1024]{2,1,0:T(8,128)(2,1)}, u32[]{:S(2)}) copy-start(bf16[1,128,1024]{2,1,0:T(8,128)(2,1)} %param.9) | copy-start | bytes 786436
  0.7 3.0 %copy-start.2 = (bf16[1,128,1024]{2,1,0:T(8,128)(2,1)S(1)}, bf16[1,128,1024]{2,1,0:T(8,128)(2,1)}, u32[]{:S(2)}) copy-start(bf16[1,128,1024]{2,1,0:T(8,128)(2,1)} %param.8) | copy-start | bytes 786436
  0.7 3.0 %copy-start.1 = (bf16[1,128,1024]{2,1,0:T(8,128)(2,1)S(1)}, bf16[1,128,1024]{2,1,0:T(8,128)(2,1)}, u32[]{:S(2)}) copy-start(bf16[1,128,1024]{2,1,0:T(8,128)(2,1)} %param.7) | copy-start | bytes 786436
where the time goes:
time: 107 us
  Pallas kernels  99.4 us (93%)
  local copies, waits for them, and re-layouts  3.7 us (3%)
  matrix products  2.03 us (2%)
    pallas_call x1, Pallas kernels, by_heads(): pl.pallas_call(lambda *refs: layer_kernel(n, *refs), out_shape=(shape((to...  99.4 us
    unnamed x15, local copies, waits for them, and re-layouts  3.63 us

commit v1 on v0

--- a/solution.py
+++ b/solution.py
@@ -260,262 +260,480 @@
     pl.semaphore_wait(barrier, len(devices))
 
 
+def swap_bits(v):
+    return 2 * lax.rem(v, 2) + v // 2
+
+
+class PlaneGather:
+    def __init__(self, buf, base, y, col, count, ss, rs, sends):
+        self.buf, self.base, self.y, self.col = buf, base, y, col
+        self.count, self.ss, self.rs, self.sends = count, ss, rs, sends
+        self.mate = col + 1 - 2 * lax.rem(col, 2)
+        self.across = lax.rem(col + 2, 4)
+        self.mate_across = lax.rem(self.mate + 2, 4)
+
+    def block(self, y, col, part=None):
+        begin = self.base(y, col) * self.count
+        if part is None:
+            return self.buf.at[rows_of(begin, self.count)]
+        half = self.count // 2
+        return self.buf.at[rows_of(begin + part * half, half)]
+
+    def send(self, slot, source, target, device):
+        copy = remote(source, target, self.ss.at[slot], self.rs.at[slot], device)
+        copy.start()
+        self.sends.append(copy)
+
+    def wait(self, slot, block):
+        remote(
+            block, block, self.ss.at[slot], self.rs.at[slot], {"fsdp": self.mate}
+        ).wait_recv()
+
+    def start(self, own):
+        half = self.count // 2
+        other = {"cp": lax.axis_index("cp") + 1 - 2 * self.y}
+        for part in range(2):
+            piece = own.at[pl.ds(part * half, half)]
+            self.send(part, piece, self.block(self.y, self.col, part), other)
+        whole = self.block(self.y, self.col)
+        self.send(2, own, whole, {"fsdp": self.across})
+        self.send(3, own, whole, {"fsdp": self.mate})
+
+    def relay_y(self, part):
+        block = self.block(1 - self.y, self.col, part)
+        self.wait(part, block)
+        self.send(4 + part, block, block, {"fsdp": self.across})
+        self.send(6 + part, block, block, {"fsdp": self.mate})
+
+    def relay_x(self):
+        block = self.block(self.y, self.across)
+        self.wait(2, block)
+        self.send(8, block, block, {"fsdp": self.mate})
+
+    def relay_diagonal(self, part):
+        block = self.block(1 - self.y, self.across, part)
+        self.wait(4 + part, block)
+        self.send(9 + part, block, block, {"fsdp": self.mate})
+
+    def wait_mate(self):
+        self.wait(3, self.block(self.y, self.mate))
+
+    def wait_mate_y(self):
+        for part in range(2):
+            self.wait(6 + part, self.block(1 - self.y, self.mate, part))
+
+    def wait_mate_x(self):
+        self.wait(8, self.block(self.y, self.mate_across))
+
+    def wait_mate_diagonal(self):
+        for part in range(2):
+            self.wait(9 + part, self.block(1 - self.y, self.mate_across, part))
+
+
 def layer_kernel(
-    n, q, k, v, up, w, allowed, proj, dq, dk, dv, wg,
-    qh, kh, vh, ups, wall, prob, att, attended, dqh, dkh, dvh, dk_sum, dv_sum, dw_sum, dw, dwr,
-    kt, vt, local_sem, heads_s, heads_r, out_s, out_r, ring_s, ring_r,
-    part_s, part_r, cross_s, cross_r, relay_s, relay_r, ws, wr,
+    n, q, k, v, up, w, order, mask, proj, dq, dk, dv, wg,
+    qh, kh, vh, ups, wall, bias, prob, dsb, att, attended, attp, ga_out, ga,
+    dqh, dkh, dvh, dw, dwr, kt, vt,
+    heads_s, heads_r, out_s, out_r, up_s, up_r, wide_s, wide_r,
+    slab_s, slab_r, chain_s, chain_r, ga_s, ga_r, attp_s, attp_r, dw_s, dw_r,
 ):
     me = lax.axis_index("cp")
     col = lax.axis_index("fsdp")
-    partner = {"fsdp": col + 1 - 2 * lax.rem(col, 2)}
-    cross_col = lax.rem(col + 2, 4)
-    cross = {"fsdp": cross_col}
+    cols = lax.axis_size("fsdp")
+    planes = n // 2
+    zed, why = me // 2, lax.rem(me, 2)
     tokens = up.shape[0]
-    half = tokens // 2
     slab = w.shape[0]
-    depth = n // 2
-    zed, why = me // 2, lax.rem(me, 2)
-    place = zed + why * (n - 1 - 2 * zed)
-
-    def at_place(offset):
-        r = lax.rem(place + offset + 2 * n, n)
-        return 2 * r + (r // depth) * (2 * n - 1 - 4 * r)
+    length = tokens * n
+    span_rows = tokens // 2
+    bf16, f32 = jnp.bfloat16, jnp.float32
+    nt = (((1,), (1,)), ((), ()))
+    home = swap_bits(col)
+    work_head = 2 * home + why
+    root = home == zed
+    pieces = chain_r.shape[0]
 
     def head_cols(d):
         return rows_of(d * HEAD, HEAD)
 
-    peers = [{"cp": lax.rem(me + i, n)} for i in range(1, n)]
-    columns = [{"fsdp": lax.rem(col + j, 4)} for j in range(1, 4)]
-    greet(peers + columns)
-
-    def chunk_ref(which, owner):
-        if which == 2:
-            return wall.at[rows_of(owner * (4 * slab) + col * slab, slab)]
-        return ups.at[rows_of(owner * tokens + which * half, half)]
-
-    def own_ref(which):
-        if which == 2:
-            return w
-        return up.at[rows_of(which * half, half)]
+    def rows(d):
+        return rows_of(d * tokens, tokens)
+
+    barrier = pltpu.get_barrier_semaphore()
+    for i in range(n):
+        for j in range(cols):
+            if i or j:
+                pl.semaphore_signal(
+                    barrier, inc=1,
+                    device_id={"cp": lax.rem(me + i, n), "fsdp": lax.rem(col + j, cols)},
+                    device_id_type=MESH,
+                )
+    pl.semaphore_wait(barrier, n * cols - 1)
 
     sends = []
-    toward = ({"cp": at_place(1)}, {"cp": at_place(-1)})
-
-    def chunks_at(step, way):
-        if step < depth:
-            return (2, 0, 1)
-        return (2, 0) if way == 0 else (1,)
-
-    def ring_start(step, way, which):
-        owner = at_place((1 - step) if way == 0 else (step - 1))
-        source = own_ref(which) if step == 1 else chunk_ref(which, owner)
-        copy = remote(
-            source, chunk_ref(which, owner),
-            ring_s.at[way, step, which], ring_r.at[way, step, which], toward[way],
-        )
-        copy.start()
-        sends.append(copy)
-
-    def ring_wait(step, way, which):
-        owner = at_place(-step if way == 0 else step)
-        block = chunk_ref(which, owner)
-        remote(
-            block, block, ring_s.at[way, step, which], ring_r.at[way, step, which], toward[way]
-        ).wait_recv()
-
-    spread = []
-
-    def spread_weight(owner, source):
-        slot = len(spread)
-        spread.append(owner)
-        block = chunk_ref(2, owner)
-        for device, ss, rs in ((cross, cross_s, cross_r), (partner, part_s, part_r)):
-            copy = remote(source, block, ss.at[slot], rs.at[slot], device)
-            copy.start()
-            sends.append(copy)
-
-    for way in range(2):
-        for which in chunks_at(1, way):
-            ring_start(1, way, which)
-    triples = ((q, qh), (k, kh), (v, vh))
-    for i in range(1, n):
-        d = lax.rem(me + i, n)
-        for t, (a, b) in enumerate(triples):
+    offsets = [n // 2]
+    for i in range(1, n // 2):
+        offsets += [n // 2 - i, n // 2 + i]
+
+    def heads_send(t, source, target):
+        for i in offsets:
+            d = lax.rem(me + i, n)
             copy = remote(
-                a.at[:, head_cols(d)], b.at[rows_of(me * tokens, tokens)],
+                source.at[:, head_cols(d)], target.at[rows(me)],
                 heads_s.at[t, i], heads_r.at[t, i], {"cp": d},
             )
             copy.start()
             sends.append(copy)
-    own = [
-        pltpu.make_async_copy(
-            a.at[:, head_cols(me)], b.at[rows_of(me * tokens, tokens)], local_sem.at[t]
-        )
-        for t, (a, b) in enumerate(triples)
-    ]
-    own.append(pltpu.make_async_copy(up, ups.at[rows_of(me * tokens, tokens)], local_sem.at[3]))
-    own.append(pltpu.make_async_copy(w, chunk_ref(2, me), local_sem.at[4]))
-    for copy in own:
-        copy.start()
-    spread_weight(me, w)
-    bf16, f32 = jnp.bfloat16, jnp.float32
-    nt = (((1,), (1,)), ((), ()))
-    near = partner["fsdp"]
-    far = lax.rem(near + 2, 4)
-
-    def relay(slot):
-        block = wall.at[rows_of(spread[slot] * (4 * slab) + cross_col * slab, slab)]
-        remote(block, block, cross_s.at[slot], cross_r.at[slot], cross).wait_recv()
-        copy = remote(block, block, relay_s.at[slot], relay_r.at[slot], partner)
-        copy.start()
-        sends.append(copy)
-
-    def weight_wait(slot):
-        for other, ss, rs in ((near, part_s, part_r), (far, relay_s, relay_r)):
-            block = wall.at[rows_of(spread[slot] * (4 * slab) + other * slab, slab)]
-            remote(block, block, ss.at[slot], rs.at[slot], partner).wait_recv()
-
-    def advance(step, chunks):
-        for which in chunks:
-            for way in range(2):
-                if which not in chunks_at(step, way):
-                    continue
-                ring_wait(step, way, which)
-                if step < depth and which in chunks_at(step + 1, way):
-                    ring_start(step + 1, way, which)
-                if which == 2:
-                    owner = at_place(-step if way == 0 else step)
-                    spread_weight(owner, chunk_ref(2, owner))
+
+    def heads_wait(t, target):
+        for i in offsets:
+            source = lax.rem(me + n - i, n)
+            block = target.at[rows(source)]
+            remote(block, block, heads_s.at[t, i], heads_r.at[t, i], {"cp": source}).wait_recv()
 
     def out_send(t, i, source, target):
         d = lax.rem(me + i, n)
-        copy = remote(
-            source.at[rows_of(d * tokens, tokens)], target.at[:, head_cols(me)],
+        return remote(
+            source.at[rows(d)], target.at[:, head_cols(me)],
             out_s.at[t, i], out_r.at[t, i], {"cp": d},
         )
-        copy.start()
-        sends.append(copy)
 
     def out_wait(t, target):
-        for i in range(1, n):
+        for i in offsets:
             source = lax.rem(me + n - i, n)
             block = target.at[:, head_cols(source)]
             remote(block, block, out_s.at[t, i], out_r.at[t, i], {"cp": source}).wait_recv()
 
-    advance(1, (2, 0, 1))
-    relay(0)
-    for i in range(1, n):
-        source = lax.rem(me + n - i, n)
-        for t, (a, b) in enumerate(triples):
-            block = b.at[rows_of(source * tokens, tokens)]
-            remote(block, block, heads_s.at[t, i], heads_r.at[t, i], {"cp": source}).wait_recv()
-    for copy in own:
-        copy.wait()
+    up_gather = PlaneGather(
+        ups, lambda y, c: c * 2 + y, why, col, tokens, up_s, up_r, sends
+    )
+    wide_gather = PlaneGather(
+        wall, lambda y, c: 2 * swap_bits(c) + y, why, col, HEAD, wide_s, wide_r, sends
+    )
+
+    mine_slab = wall.at[rows_of(me * HEAD + col * slab, slab)]
+    slab_copy = remote(
+        w, mine_slab, slab_s.at[0], slab_r.at[col], {"fsdp": swap_bits(zed)}
+    )
+
+    @pl.when(jnp.logical_not(root))
+    def _():
+        slab_copy.start()
+
+    heads_send(0, k, kh)
+    up_gather.start(up)
+
+    @pl.when(root)
+    def _():
+        wall[rows_of(me * HEAD + col * slab, slab)] = w[...]
+        for j in range(1, cols):
+            other = lax.rem(col + j, cols)
+            block = wall.at[rows_of(me * HEAD + other * slab, slab)]
+            remote(block, block, slab_s.at[0], slab_r.at[other], {"fsdp": other}).wait_recv()
+
+    piece_rows = HEAD // pieces
+    rising = jnp.logical_and(zed >= home, zed < planes - 1)
+    falling = jnp.logical_and(zed <= home, zed > 0)
+
+    def chain_copy(p, way):
+        block = wall.at[rows_of(work_head * HEAD + p * piece_rows, piece_rows)]
+        target = me + 2 if way == 0 else me - 2
+        return remote(block, block, chain_s.at[way, p], chain_r.at[p], {"cp": target})
+
+    def chain_forward(p):
+        @pl.when(rising)
+        def _():
+            chain_copy(p, 0).start()
+
+        @pl.when(falling)
+        def _():
+            chain_copy(p, 1).start()
+
+    @pl.when(root)
+    def _():
+        for p in range(pieces):
+            chain_forward(p)
+
+    heads_send(1, q, qh)
+    heads_send(2, v, vh)
+    for source, target in ((k, kh), (q, qh), (v, vh)):
+        target[rows(me)] = source[:, head_cols(me)]
+    ups[rows(col * 2 + why)] = up[...]
+
+    spans = order.shape[0]
+    order_row = jnp.broadcast_to(order[...].reshape(1, spans), (spans, spans))
+    place = lax.broadcasted_iota(jnp.int32, (spans, spans), 0)
+    at_place = (order_row == place).astype(f32).astype(bf16)
+    row = lax.broadcasted_iota(jnp.int32, (length, spans), 0)
+    begin = lax.broadcasted_iota(jnp.int32, (length, spans), 1) * span_rows
+    member = jnp.logical_and(row >= begin, row < begin + span_rows).astype(f32).astype(bf16)
+    row_t = lax.broadcasted_iota(jnp.int32, (spans, length), 1)
+    begin_t = lax.broadcasted_iota(jnp.int32, (spans, length), 0) * span_rows
+    member_t = jnp.logical_and(row_t >= begin_t, row_t < begin_t + span_rows)
+    member_t = member_t.astype(f32).astype(bf16)
+    placed = lax.dot_general(member, at_place, nt, preferred_element_type=f32)
+    placed_t = jnp.dot(at_place, member_t, preferred_element_type=f32)
+    shift = lax.broadcasted_iota(jnp.int32, (length, spans), 1) * span_rows
+    shift_t = lax.broadcasted_iota(jnp.int32, (spans, length), 0) * span_rows
+    within = (row - begin).astype(f32) * member.astype(f32)
+    within_t = (row_t - begin_t).astype(f32) * member_t.astype(f32)
+    key_pos = (placed * shift.astype(f32) + within).sum(1, keepdims=True)
+    query_pos = (placed_t * shift_t.astype(f32) + within_t).sum(0, keepdims=True)
+    key_side = lax.dot_general(
+        placed.astype(bf16), mask[...].astype(f32).astype(bf16), nt, preferred_element_type=f32
+    ).astype(bf16)
+    placed_low = placed_t.astype(bf16)
+    for o in range(n):
+        part = slice(o * tokens, (o + 1) * tokens)
+        seen = jnp.dot(key_side, placed_low[:, part], preferred_element_type=f32)
+        allowed = jnp.logical_and(seen > 0.5, key_pos <= query_pos[:, part])
+        bias[:, part] = jnp.where(allowed, 0.0, lowest)
+
+    def chain_relay(p):
+        @pl.when(jnp.logical_not(root))
+        def _():
+            block = wall.at[rows_of(work_head * HEAD + p * piece_rows, piece_rows)]
+            remote(block, block, chain_s.at[0, p], chain_r.at[p], {"cp": me}).wait_recv()
+            chain_forward(p)
+
+    heads_wait(0, kh)
     kt[...] = kh[...].astype(f32).T.astype(bf16)
-    vt[...] = vh[...].astype(f32).T.astype(bf16)
-    dk_sum[...] = jnp.zeros_like(dk_sum)
-    dv_sum[...] = jnp.zeros_like(dv_sum)
-    dw_sum[...] = jnp.zeros_like(dw_sum)
-
-    def forward(o, carry):
-        rows = rows_of(o * tokens, tokens)
-        scores = lax.dot_general(kh[...], qh[rows], nt, preferred_element_type=f32) * (1.0 / HEAD)
-        scores = jnp.where(allowed[:, rows].astype(f32) > 0.5, scores, lowest)
+    for p in range(pieces // 2):
+        chain_relay(p)
+    up_gather.relay_y(0)
+    for p in range(pieces // 2, pieces):
+        chain_relay(p)
+    up_gather.relay_x()
+    heads_wait(1, qh)
+
+    def soft(o, carry):
+        part = rows(o)
+        scores = lax.dot_general(kh[...], qh[part], nt, preferred_element_type=f32) * (1.0 / HEAD)
+        scores = scores + bias[:, part]
         terms = jnp.exp(scores - scores.max(0, keepdims=True))
         probability = terms * (1.0 / terms.sum(0, keepdims=True))
-        prob[:, rows] = probability
-        att_t = jnp.dot(vt[...], probability.astype(bf16), preferred_element_type=f32)
-        att[rows] = att_t.T.astype(bf16)
+        prob[:, part] = probability.astype(bf16)
         return carry
 
-    lax.fori_loop(0, n, forward, 0)
-    weight_wait(0)
-    for i in range(1, n):
-        out_send(0, i, att, attended)
-    attended[:, head_cols(me)] = att[rows_of(me * tokens, tokens)]
-
-    def backward(o):
-        rows = rows_of(o * tokens, tokens)
-        up_rows = ups[rows]
-        ga = lax.dot_general(
-            up_rows, wall[rows_of(me * HEAD, HEAD)], nt, preferred_element_type=f32
+    lax.fori_loop(0, n // 2, soft, 0)
+    up_gather.relay_y(1)
+    wide_gather.start(wall.at[rows_of(work_head * HEAD, HEAD)])
+    lax.fori_loop(n // 2, n, soft, 0)
+
+    def ga_copy(j, s):
+        return remote(
+            ga_out.at[rows_of(s * 2 * tokens, 2 * tokens)],
+            ga.at[rows_of(zed * 2 * tokens, 2 * tokens)],
+            ga_s.at[j], ga_r.at[zed], {"cp": work_head, "fsdp": s},
+        )
+
+    def ga_group(j, s):
+        part = rows_of(s * 2 * tokens, 2 * tokens)
+        result = lax.dot_general(
+            ups[part], wall[rows_of(work_head * HEAD, HEAD)], nt, preferred_element_type=f32
         ).astype(bf16)
-        att_rows = att[rows]
-        delta = (att_rows.astype(f32) * ga.astype(f32)).T.sum(0, keepdims=True)
-        dprob = lax.dot_general(vh[...], ga, nt, preferred_element_type=f32)
-        probability = prob[:, rows]
-        ds = (probability * (dprob - delta) * (1.0 / HEAD)).astype(bf16)
-        dqh[rows] = jnp.dot(kt[...], ds, preferred_element_type=f32).T.astype(bf16)
-        dk_sum[...] += jnp.dot(ds, qh[rows], preferred_element_type=f32)
-        dv_sum[...] += jnp.dot(probability.astype(bf16), ga, preferred_element_type=f32)
-        dw_sum[...] += lax.dot_general(
-            att_rows, up_rows, (((0,), (0,)), ((), ())), preferred_element_type=f32
-        )
-
-    def query_send(o):
-        i = lax.rem(o + n - me, n)
-        copy = remote(
-            dqh.at[rows_of(o * tokens, tokens)], dq.at[:, head_cols(me)],
-            out_s.at[3, i], out_r.at[3, i], {"cp": o},
-        )
+        ga_out[part] = result
+        if j == 0:
+            @pl.when(root)
+            def _():
+                ga[rows_of(zed * 2 * tokens, 2 * tokens)] = result
+
+            @pl.when(jnp.logical_not(root))
+            def _():
+                ga_copy(j, s).start()
+        else:
+            copy = ga_copy(j, s)
+            copy.start()
+            sends.append(copy)
+
+    ga_group(0, col)
+    up_gather.wait_mate()
+    up_gather.wait_mate_y()
+    ga_group(1, up_gather.mate)
+    heads_wait(2, vh)
+    vt[...] = vh[...].astype(f32).T.astype(bf16)
+
+    def attend(o, carry):
+        part = rows_of(o * 2 * tokens, 2 * tokens)
+        att_t = jnp.dot(vt[...], prob[:, part], preferred_element_type=f32)
+        att[part] = att_t.T.astype(bf16)
+        return carry
+
+    lax.fori_loop(0, n // 2, attend, 0)
+    for i in offsets:
+        copy = out_send(0, i, att, attended)
         copy.start()
         sends.append(copy)
-
-    backward(me)
-    for step in range(2, depth + 1):
-        advance(step, (2, 0))
-        if step > 2:
-            for offset in (2 - step, step - 2):
-                query_send(at_place(offset))
-        relay(2 * step - 3)
-        backward(at_place(1 - step))
-        advance(step, (1,))
-        relay(2 * step - 2)
-        backward(at_place(step - 1))
-    backward(at_place(depth))
-    dkh[...] = dk_sum[...].astype(bf16)
-    dvh[...] = dv_sum[...].astype(bf16)
-    dw[...] = dw_sum[...].astype(bf16)
-    triples_out = ((dkh, dk), (dvh, dv), (dqh, dq))
-    mine = rows_of(me * tokens, tokens)
-    for t, (a, b) in enumerate(triples_out):
-        b[:, head_cols(me)] = a[mine]
-        if t < 2:
-            for i in range(1, n):
-                out_send(t + 1, i, a, b)
-    for offset in (1 - depth, depth - 1, depth):
-        query_send(at_place(offset))
-    for j in range(1, 4):
-        g = lax.rem(col + j, 4)
-        copy = remote(dw.at[rows_of(g * slab, slab)], dwr.at[j], ws.at[j], wr.at[j], {"fsdp": g})
+    attended[:, head_cols(me)] = att[rows(me)]
+    up_gather.relay_diagonal(0)
+    up_gather.relay_diagonal(1)
+    ga_group(2, up_gather.across)
+    up_gather.wait_mate_x()
+    up_gather.wait_mate_diagonal()
+    ga_group(3, up_gather.mate_across)
+    wide_gather.relay_y(0)
+    wide_gather.relay_x()
+    wide_gather.relay_y(1)
+
+    out_wait(0, attended)
+    own_rows = (col * 2 + why) * tokens
+    for i in range(2):
+        for j in range(cols):
+            if i == 0 and j == 0:
+                attp[rows_of(own_rows, tokens)] = attended[:, head_cols(work_head)]
+                continue
+            other_y = lax.rem(why + i, 2)
+            other_col = lax.rem(col + j, cols)
+            head = 2 * swap_bits(other_col) + other_y
+            copy = remote(
+                attended.at[:, head_cols(head)], attp.at[rows_of(own_rows, tokens)],
+                attp_s.at[i * cols + j], attp_r.at[i * cols + j],
+                {"cp": zed * 2 + other_y, "fsdp": other_col},
+            )
+            copy.start()
+            sends.append(copy)
+
+    for j in range(planes):
+        source = lax.rem(zed + j, planes)
+        block = ga.at[rows_of(source * 2 * tokens, 2 * tokens)]
+        arrived = remote(block, block, ga_s.at[0], ga_r.at[source], {"cp": me})
+        if j == 0:
+            @pl.when(jnp.logical_not(root))
+            def _():
+                arrived.wait_recv()
+        else:
+            arrived.wait_recv()
+
+    def value_step(o, carry):
+        part = rows_of(o * 2 * tokens, 2 * tokens)
+        dvh[part] = jnp.dot(prob[part], ga[...], preferred_element_type=f32).astype(bf16)
+        return carry
+
+    lax.fori_loop(0, n // 2, value_step, 0)
+    for i in offsets:
+        copy = out_send(2, i, dvh, dv)
         copy.start()
         sends.append(copy)
-    relay(len(spread) - 1)
-    for slot in range(1, len(spread)):
-        weight_wait(slot)
-    out_wait(0, attended)
+    dv[:, head_cols(me)] = dvh[rows(me)]
+
+    def backward(i, carry):
+        o = lax.rem(me + i, n)
+        part = rows(o)
+        ga_rows = ga[part]
+        delta = (att[part].astype(f32) * ga_rows.astype(f32)).T.sum(0, keepdims=True)
+        dprob = lax.dot_general(vh[...], ga_rows, nt, preferred_element_type=f32)
+        ds = (prob[:, part].astype(f32) * ((dprob - delta) * (1.0 / HEAD))).astype(bf16)
+        dsb[:, part] = ds
+        dqh[part] = jnp.dot(kt[...], ds, preferred_element_type=f32).T.astype(bf16)
+
+        @pl.when(i > 0)
+        def _():
+            out_send(3, i, dqh, dq).start()
+
+        return carry
+
+    lax.fori_loop(0, n, lambda i, c: backward(lax.rem(i + n // 2, n), c), 0)
+    dq[:, head_cols(me)] = dqh[rows(me)]
+
+    def key_step(o, carry):
+        part = rows_of(o * 2 * tokens, 2 * tokens)
+        dkh[part] = jnp.dot(dsb[part], qh[...], preferred_element_type=f32).astype(bf16)
+        return carry
+
+    lax.fori_loop(0, n // 2, key_step, 0)
+    for i in offsets:
+        copy = out_send(1, i, dkh, dk)
+        copy.start()
+        sends.append(copy)
+    dk[:, head_cols(me)] = dkh[rows(me)]
+
+    for i in range(2):
+        for j in range(cols):
+            if i == 0 and j == 0:
+                continue
+            other_y = lax.rem(why + 2 - i, 2)
+            other_col = lax.rem(col + cols - j, cols)
+            block = attp.at[rows_of((other_col * 2 + other_y) * tokens, tokens)]
+            remote(
+                block, block, attp_s.at[i * cols + j], attp_r.at[i * cols + j], {"cp": me}
+            ).wait_recv()
+    att_t = attp[...].astype(f32).T.astype(bf16)
     width = math.gcd(proj.shape[1], 512)
+    for i in range(proj.shape[1] // width):
+        part = slice(i * width, (i + 1) * width)
+        dw[:, part] = jnp.dot(att_t, ups[:, part], preferred_element_type=f32).astype(bf16)
+
+    def dw_copy(j):
+        s = lax.rem(col + j, cols)
+        return remote(
+            dw.at[rows_of(s * slab, slab)], dwr.at[zed], dw_s.at[j], dw_r.at[zed],
+            {"cp": work_head, "fsdp": s},
+        )
+
+    @pl.when(root)
+    def _():
+        dwr[zed] = dw[rows_of(col * slab, slab)]
+
+    @pl.when(jnp.logical_not(root))
+    def _():
+        dw_copy(0).start()
+
+    for j in range(1, cols):
+        copy = dw_copy(j)
+        copy.start()
+        sends.append(copy)
+
+    wide_gather.relay_diagonal(0)
+    wide_gather.relay_diagonal(1)
+    wide_gather.wait_mate()
+    wide_gather.wait_mate_y()
+    wide_gather.wait_mate_x()
+    wide_gather.wait_mate_diagonal()
 
     def project(i, carry):
-        cols = rows_of(i * width, width)
-        proj[:, cols] = jnp.dot(
-            attended[...], wall[:, cols], preferred_element_type=f32
+        part = rows_of(i * width, width)
+        proj[:, part] = jnp.dot(
+            attended[...], wall[:, part], preferred_element_type=f32
         ).astype(bf16)
         return carry
 
     lax.fori_loop(0, proj.shape[1] // width, project, 0)
-    for j in range(1, 4):
-        block = dwr.at[j]
-        remote(block, block, ws.at[j], wr.at[j], columns[j - 1]).wait_recv()
-    total = dw[rows_of(col * slab, slab)].astype(f32)
-    for j in range(1, 4):
+    for j in range(planes):
+        source = lax.rem(zed + j, planes)
+        block = dwr.at[source]
+        arrived = remote(block, block, dw_s.at[0], dw_r.at[source], {"cp": me})
+        if j == 0:
+            @pl.when(jnp.logical_not(root))
+            def _():
+                arrived.wait_recv()
+        else:
+            arrived.wait_recv()
+    total = dwr[0].astype(f32)
+    for j in range(1, planes):
         total = total + dwr[j].astype(f32)
     wg[...] = total
-    for t, (a, b) in enumerate(triples_out):
-        out_wait(t + 1, b)
+    out_wait(2, dv)
+    out_wait(3, dq)
+    out_wait(1, dk)
     for copy in sends:
         copy.wait_send()
+    for i in offsets:
+        out_send(3, i, dqh, dq).wait_send()
+
+    @pl.when(jnp.logical_not(root))
+    def _():
+        slab_copy.wait_send()
+        ga_copy(0, col).wait_send()
+        dw_copy(0).wait_send()
+
+    for p in range(pieces):
+        @pl.when(rising)
+        def _():
+            chain_copy(p, 0).wait_send()
+
+        @pl.when(falling)
+        def _():
+            chain_copy(p, 1).wait_send()
 
 
 def by_heads(query_states, key_states, value_states, span_order, block_mask, output_weight, upstream):
@@ -525,50 +743,42 @@
     length = tokens * n
     model = upstream.shape[2]
     slab = output_weight.shape[0]
-    span_rows = tokens // 2
     bf16, f32 = jnp.bfloat16, jnp.float32
     shape = jax.ShapeDtypeStruct
     vmem = pl.BlockSpec(memory_space=pltpu.VMEM)
     dma = pltpu.SemaphoreType.DMA
-    half = n // 2
-    positions = (
-        span_order[:, None] * span_rows + jnp.arange(span_rows, dtype=jnp.int32)[None, :]
-    ).reshape(-1)
-    spans = span_order.shape[0]
-    member = (
-        jnp.arange(length, dtype=jnp.int32)[:, None] // span_rows
-        == jnp.arange(spans, dtype=jnp.int32)[None, :]
-    ).astype(bf16)
-    span_ok = storage_mask(span_order, block_mask).astype(bf16)
-    key_side = lax.dot_general(member, span_ok, (((1,), (1,)), ((), ())), preferred_element_type=bf16)
-    seen = lax.dot_general(key_side, member, (((1,), (1,)), ((), ())), preferred_element_type=f32)
-    allowed = ((seen > 0.5) & (positions[:, None] <= positions[None, :])).astype(bf16)
+    planes = n // 2
+    pieces = 4
     head_array = pltpu.VMEM((length, HEAD), bf16)
-    head_sum = pltpu.VMEM((length, HEAD), f32)
+    square = pltpu.VMEM((length, length), bf16)
     projected, dq, dk, dv, weight_gradient = pl.pallas_call(
         lambda *refs: layer_kernel(n, *refs),
         out_shape=(shape((tokens, model), bf16),)
         + (shape((tokens, width), bf16),) * 3
         + (shape((slab, model), f32),),
-        in_specs=[vmem] * 6,
+        in_specs=[vmem] * 7,
         out_specs=(vmem,) * 5,
         scratch_shapes=[
             head_array, head_array, head_array,
             pltpu.VMEM((length, model), bf16), pltpu.VMEM((width, model), bf16),
-            pltpu.VMEM((length, length), f32), head_array, pltpu.VMEM((tokens, width), bf16),
-            head_array, head_array, head_array, head_sum, head_sum,
-            pltpu.VMEM((HEAD, model), f32), pltpu.VMEM((HEAD, model), bf16),
-            pltpu.VMEM((m, slab, model), bf16),
+            pltpu.VMEM((length, length), f32), square, square,
+            head_array, pltpu.VMEM((tokens, width), bf16), head_array, head_array, head_array,
+            head_array, head_array, head_array,
+            pltpu.VMEM((HEAD, model), bf16), pltpu.VMEM((planes, slab, model), bf16),
             pltpu.VMEM((HEAD, length), bf16), pltpu.VMEM((HEAD, length), bf16),
-            dma((5,)), dma((3, n)), dma((3, n)), dma((4, n)), dma((4, n)),
-            dma((2, half + 1, 3)), dma((2, half + 1, 3)),
-        ]
-        + [dma((n,))] * 6 + [dma((m,))] * 2,
+            dma((3, n)), dma((3, n)), dma((4, n)), dma((4, n)),
+            dma((11,)), dma((11,)), dma((11,)), dma((11,)),
+            dma((1,)), dma((m,)), dma((2, pieces)), dma((pieces,)),
+            dma((m,)), dma((planes,)), dma((2 * m,)), dma((2 * m,)), dma((m,)), dma((planes,)),
+        ],
         compiler_params=pltpu.CompilerParams(
             collective_id=0, has_side_effects=True, vmem_limit_bytes=48 << 20
         ),
         name="layer",
-    )(query_states[0], key_states[0], value_states[0], upstream[0], output_weight, allowed)
+    )(
+        query_states[0], key_states[0], value_states[0], upstream[0], output_weight,
+        span_order, block_mask,
+    )
     return (projected[None], dq[None], dk[None], dv[None], weight_gradient)
 
 

time: 107 us -> 96.8 us (0.905)
  the two profiles are of different devices: /device:TPU:0 before, /device:TPU:7 now
where the time goes in v1:
time: 96.8 us; the launch traced here: 96.5 us
  Pallas kernels  86.1 us (89%)
  local copies, waits for them, and re-layouts  9.74 us (10%)
    pallas_call x1, Pallas kernels, by_heads(): pl.pallas_call(lambda *refs: layer_kernel(n, *refs), out_shape=(shape((to...  86.1 us
    unnamed x19, local copies, waits for them, and re-layouts  9.74 us

profile of v1, /device:TPU:7, one launch (start us, length us, event | category | flops | bytes accessed | tf_op | source)
XLA Modules:
  0.0 96.5 jit_solution(1911391667065215340)
XLA Ops:
  0.6 0.0 copy-start.6
  0.6 0.6 copy-done.6
  1.3 0.0 copy-start
  1.3 1.0 %copy-done = bf16[1,128,2048]{2,1,0:T(8,128)(2,1)S(1)} copy-done((bf16[1,128,2048]{2,1,0:T(8,128)(2,1)S(1)}, bf16[1,128,2048]{2,1,0:T(8,128)(2,1)}, u32[]{:S(2)}) %copy-start) | copy-done | bytes 524312
  2.3 0.0 copy-start.1
  2.3 0.9 copy-done.1
  3.3 0.0 copy-start.2
  3.3 0.9 copy-done.2
  4.2 0.0 copy-start.3
  4.2 0.9 copy-done.3
  5.2 0.0 copy-start.4
  5.2 0.9 copy-done.4
  6.1 0.0 copy-start.5
  6.1 0.7 copy-done.5
  6.8 86.1 %layer.1 = (bf16[128,2048]{1,0:T(8,128)(2,1)S(1)}, bf16[128,1024]{1,0:T(8,128)(2,1)S(1)}, bf16[128,1024]{1,0:T(8,128)(2,1)S(1)}, bf16[128,1024]{1,0:T(8,128)(2,1)S(1)}, f32[32,2048]{1,0:T(8,128)S(1)}) custom-call(bf16[128,1024]{1,0:T(8,128)(2,1)S(1)} %bitcast.13, bf16[128,1024]{1,0:T(8,128)(2,1)S(1)} %bitcast.14, bf16[128,1024]{1,0:T(8,128)(2,1)S(1)} %bitcast.15, ...), custom_call_target="tpu_custom_call" | custom-call | tf_op jit(solution)/shard_map/layer/pallas_call | solution.py:754
  92.8 0.8 copy.17
  93.6 0.7 copy.18
  94.3 0.7 copy.19
  95.1 0.7 copy.20
  95.8 0.7 copy.21
Async XLA Ops:
  0.6 0.7 copy-start.6
  1.3 1.0 %copy-start = (bf16[1,128,2048]{2,1,0:T(8,128)(2,1)S(1)}, bf16[1,128,2048]{2,1,0:T(8,128)(2,1)}, u32[]{:S(2)}) copy-start(bf16[1,128,2048]{2,1,0:T(8,128)(2,1)} %param.13) | copy-start | bytes 1572868
  2.3 0.9 copy-start.1
  3.3 0.9 copy-start.2
  4.2 0.9 copy-start.3
  5.2 0.9 copy-start.4
  6.1 0.7 copy-start.5

commit v2 on v1

v2 whole, which is shorter than its diff:
```python
import math

import jax
import jax.numpy as jnp
from jax import lax
from jax.experimental import pallas as pl
from jax.experimental.pallas import tpu as pltpu
from jax.sharding import PartitionSpec as P

HEADS = 8
HEAD = 128


lowest = -1e30


def split_heads(row_block):
    return row_block.reshape(row_block.shape[0], HEADS, HEAD)


def pair_scores(query_rows, key_rows):
    return jnp.einsum(
        "qhd,khd->hqk",
        split_heads(query_rows),
        split_heads(key_rows),
        preferred_element_type=jnp.float32,
    ) * (1.0 / HEAD)


def storage_mask(span_order, block_mask):
    span_count = span_order.shape[0]
    onehot = (span_order[:, None] == jnp.arange(span_count, dtype=jnp.int32)[None, :]).astype(
        jnp.float32
    )
    permuted = jnp.dot(jnp.dot(onehot, block_mask.astype(jnp.float32)), onehot.T)
    return permuted > 0.5


def allowed_block(span_ok, positions, query_begin, query_total, key_begin, key_total, span_rows):
    span_sub = lax.dynamic_slice(
        span_ok,
        (query_begin // span_rows, key_begin // span_rows),
        (query_total // span_rows, key_total // span_rows),
    )
    spread = jnp.broadcast_to(
        span_sub[:, None, :, None],
        (query_total // span_rows, span_rows, key_total // span_rows, span_rows),
    )
    spread = spread.reshape(query_total, key_total)
    query_pos = lax.dynamic_slice_in_dim(positions, query_begin, query_total)
    key_pos = lax.dynamic_slice_in_dim(positions, key_begin, key_total)
    return spread & (key_pos[None, :] <= query_pos[:, None])


def local_terms(query_rows, grad_rows, log_rows, delta_rows, key_rows, value_rows, allowed):
    scores = pair_scores(query_rows, key_rows)
    probability = jnp.where(allowed[None], jnp.exp(scores - log_rows[..., None]), 0.0)
    dprob = jnp.einsum(
        "qhd,khd->hqk",
        split_heads(grad_rows),
        split_heads(value_rows),
        preferred_element_type=jnp.float32,
    )
    dscores = (probability * (dprob - delta_rows[..., None]) * (1.0 / HEAD)).astype(jnp.bfloat16)
    return (probability, dscores)


def local(query_states, key_states, value_states, span_order, block_mask, output_weight, upstream):
    query_rows = query_states[0]
    key_local = key_states[0]
    value_local = value_states[0]
    upstream_rows = upstream[0]
    tokens = query_rows.shape[0]
    span_rows = tokens // 2
    positions = (
        span_order[:, None] * span_rows + jnp.arange(span_rows, dtype=jnp.int32)[None, :]
    ).reshape(-1)
    span_ok = storage_mask(span_order, block_mask)
    own_start = lax.axis_index("cp") * tokens
    key_all, value_all = (
        lax.all_gather(key_local, "cp", axis=0, tiled=True),
        lax.all_gather(value_local, "cp", axis=0, tiled=True),
    )
    weight = lax.all_gather(output_weight, ("cp", "fsdp"), axis=0, tiled=True)
    length = key_all.shape[0]
    key_block = math.gcd(length, 512)
    block_count = length // key_block
    block_steps = jnp.arange(block_count, dtype=jnp.int32)

    def stats_step(running, step_index):
        key_begin = step_index * key_block
        key_rows = lax.dynamic_slice_in_dim(key_all, key_begin, key_block)
        allowed = allowed_block(
            span_ok, positions, own_start, tokens, key_begin, key_block, span_rows
        )
        maxima, totals = running
        scores = pair_scores(query_rows, key_rows)
        masked = jnp.where(allowed[None], scores, lowest)
        new_max = jnp.maximum(maxima, masked.max(-1))
        exp_terms = jnp.where(allowed[None], jnp.exp(scores - new_max[..., None]), 0.0)
        return ((new_max, totals * jnp.exp(maxima - new_max) + exp_terms.sum(-1)), None)

    stat_start = (
        jnp.full((HEADS, tokens), lowest, jnp.float32),
        jnp.zeros((HEADS, tokens), jnp.float32),
    )
    (maxima, totals), _ = lax.scan(stats_step, stat_start, block_steps)
    log_total = maxima + jnp.log(totals)

    def output_step(attn_sum, step_index):
        key_begin = step_index * key_block
        key_rows = lax.dynamic_slice_in_dim(key_all, key_begin, key_block)
        value_rows = lax.dynamic_slice_in_dim(value_all, key_begin, key_block)
        allowed = allowed_block(
            span_ok, positions, own_start, tokens, key_begin, key_block, span_rows
        )
        scores = pair_scores(query_rows, key_rows)
        probability = jnp.where(allowed[None], jnp.exp(scores - log_total[..., None]), 0.0)
        return (
            attn_sum
            + jnp.einsum(
                "hqk,khd->qhd",
                probability.astype(jnp.bfloat16),
                split_heads(value_rows),
                preferred_element_type=jnp.float32,
            ),
            None,
        )

    zero_heads = jnp.zeros((tokens, HEADS, HEAD), jnp.float32)
    attn_sum, _ = lax.scan(output_step, zero_heads, block_steps)
    attended = lax.optimization_barrier(attn_sum.reshape(tokens, -1).astype(jnp.bfloat16))
    projected = jnp.dot(attended, weight, preferred_element_type=jnp.float32).astype(jnp.bfloat16)
    grad_attended = lax.dot_general(
        upstream_rows, weight, (((1,), (1,)), ((), ())), preferred_element_type=jnp.float32
    ).astype(jnp.bfloat16)
    grad_attended = lax.optimization_barrier(grad_attended)
    weight_term = lax.dot_general(
        attended, upstream_rows, (((0,), (0,)), ((), ())), preferred_element_type=jnp.float32
    )
    row_delta = (
        (grad_attended.astype(jnp.float32) * attended.astype(jnp.float32))
        .reshape(tokens, HEADS, HEAD)
        .sum(-1)
    )
    delta_heads = row_delta.T

    def query_step(grad_sum, step_index):
        key_begin = step_index * key_block
        key_rows = lax.dynamic_slice_in_dim(key_all, key_begin, key_block)
        value_rows = lax.dynamic_slice_in_dim(value_all, key_begin, key_block)
        allowed = allowed_block(
            span_ok, positions, own_start, tokens, key_begin, key_block, span_rows
        )
        probability, dscores = local_terms(
            query_rows, grad_attended, log_total, delta_heads, key_rows, value_rows, allowed
        )
        return (
            grad_sum
            + jnp.einsum(
                "hqk,khd->qhd", dscores, split_heads(key_rows), preferred_element_type=jnp.float32
            ),
            None,
        )

    query_sum, _ = lax.scan(query_step, zero_heads, block_steps)
    query_gradient = query_sum.reshape(tokens, -1).astype(jnp.bfloat16)
    log_all, delta_all = (
        lax.all_gather(log_total.T, "cp", axis=0, tiled=True),
        lax.all_gather(row_delta, "cp", axis=0, tiled=True),
    )
    sums_now = (zero_heads, zero_heads)
    query_piece = lax.all_gather(query_rows, "cp", axis=0, tiled=True)
    grad_piece = lax.all_gather(grad_attended, "cp", axis=0, tiled=True)
    row_count = query_piece.shape[0]
    sources = row_count // tokens
    group_size = math.gcd(sources, max(1, 512 // tokens))
    group_rows = group_size * tokens

    def group_step(running, step_index):
        offset = step_index * group_rows
        query_group = lax.dynamic_slice_in_dim(query_piece, offset, group_rows)
        grad_group = lax.dynamic_slice_in_dim(grad_piece, offset, group_rows)
        log_group = lax.dynamic_slice_in_dim(log_all, offset, group_rows).T
        delta_group = lax.dynamic_slice_in_dim(delta_all, offset, group_rows).T
        allowed = allowed_block(
            span_ok, positions, offset, group_rows, own_start, tokens, span_rows
        )
        key_sum, value_sum = running
        probability, dscores = local_terms(
            query_group, grad_group, log_group, delta_group, key_local, value_local, allowed
        )
        probability_low = probability.astype(jnp.bfloat16).reshape(
            HEADS, group_size, tokens, tokens
        )
        dscores_group = dscores.reshape(HEADS, group_size, tokens, tokens)
        qsplit = query_group.reshape(group_size, tokens, HEADS, HEAD)
        gsplit = grad_group.reshape(group_size, tokens, HEADS, HEAD)
        key_part = jnp.einsum(
            "hgqk,gqhd->gkhd", dscores_group, qsplit, preferred_element_type=jnp.float32
        ).astype(jnp.bfloat16)
        value_part = jnp.einsum(
            "hgqk,gqhd->gkhd", probability_low, gsplit, preferred_element_type=jnp.float32
        ).astype(jnp.bfloat16)
        key_part, value_part = lax.optimization_barrier((key_part, value_part))
        return (
            (
                key_sum + key_part.astype(jnp.float32).sum(0),
                value_sum + value_part.astype(jnp.float32).sum(0),
            ),
            None,
        )

    sums_now, _ = lax.scan(group_step, sums_now, jnp.arange(sources // group_size, dtype=jnp.int32))
    key_sum, value_sum = sums_now
    key_gradient = key_sum.reshape(tokens, -1).astype(jnp.bfloat16)
    value_gradient = value_sum.reshape(tokens, -1).astype(jnp.bfloat16)
    cycle_count = lax.axis_size("cp")
    batch_count = lax.axis_size("fsdp")
    slab_rows = weight_term.shape[0] // (cycle_count * batch_count)
    reordered = weight_term.reshape(cycle_count, batch_count, slab_rows, -1).transpose(1, 0, 2, 3)
    reordered = reordered.reshape(weight_term.shape[0], -1)
    partial_batch = lax.psum_scatter(
        reordered.astype(jnp.bfloat16), "fsdp", scatter_dimension=0, tiled=True
    )
    weight_gradient = lax.psum_scatter(partial_batch, "cp", scatter_dimension=0, tiled=True).astype(
        jnp.float32
    )
    return (
        projected[None],
        query_gradient[None],
        key_gradient[None],
        value_gradient[None],
        weight_gradient,
    )


MESH = pl.DeviceIdType.MESH


def remote(src, dst, send_sem, recv_sem, device):
    return pltpu.make_async_remote_copy(
        src_ref=src,
        dst_ref=dst,
        send_sem=send_sem,
        recv_sem=recv_sem,
        device_id=device,
        device_id_type=MESH,
    )


def rows_of(begin, count):
    return pl.ds(pl.multiple_of(begin, count), count)


def greet(devices):
    barrier = pltpu.get_barrier_semaphore()
    for device in devices:
        pl.semaphore_signal(barrier, inc=1, device_id=device, device_id_type=MESH)
    pl.semaphore_wait(barrier, len(devices))


def layer_kernel(
    n, q_in, k_in, v_in, up_in, w_in, order_in, mask_in, proj, dq, dk, dv, wg,
    q, k, v, up, w, order, mask, load,
    qh, kh, vh, ups, wall, bias, prob, dsb, att, attended, attp, ga_out, ga,
    dqh, dkh, dvh, dw, dwx, dwz, dwr, kt, vt,
    heads_s, heads_r, out_s, out_r, up_s, up_r, wide_s, wide_r,
    slab_s, slab_r, chain_s, chain_r, side_s, side_r, ga_s, ga_r, attp_s, attp_r,
    dwx_s, dwx_r, dw_s, dw_r,
):
    me = lax.axis_index("cp")
    col = lax.axis_index("fsdp")
    cols = lax.axis_size("fsdp")
    planes = n // 2
    zed, why = me // 2, lax.rem(me, 2)
    ex, core = col // 2, lax.rem(col, 2)
    mate = {"fsdp": 2 * ex + 1 - core}
    across = {"fsdp": 2 * (1 - ex) + core}
    beside = {"cp": 2 * zed + 1 - why}
    tokens = up.shape[0]
    slab = w.shape[0]
    length = tokens * n
    span_rows = tokens // 2
    bf16, f32 = jnp.bfloat16, jnp.float32
    nt = (((1,), (1,)), ((), ()))
    home = 2 * core + ex
    root = home == zed
    keeper = core == zed // 2
    pieces = chain_r.shape[0]
    piece_rows = HEAD // pieces

    def spot(y, plane):
        return y * planes + plane

    def cols_at(place):
        return rows_of(place * HEAD, HEAD)

    def head_cols(d):
        return rows_of(d * HEAD, HEAD)

    def rows(d):
        return rows_of(d * tokens, tokens)

    def two_rows(d):
        return rows_of(d * 2 * tokens, 2 * tokens)

    pairs = (
        (k_in, k), (up_in, up), (w_in, w), (q_in, q), (v_in, v), (order_in, order), (mask_in, mask)
    )
    loads = [pltpu.make_async_copy(a, b, load.at[t]) for t, (a, b) in enumerate(pairs)]
    for copy in loads:
        copy.start()
    barrier = pltpu.get_barrier_semaphore()
    for i in range(n):
        for j in range(cols):
            if i or j:
                pl.semaphore_signal(
                    barrier, inc=1,
                    device_id={"cp": lax.rem(me + i, n), "fsdp": lax.rem(col + j, cols)},
                    device_id_type=MESH,
                )
    for copy in loads:
        copy.wait()
    pl.semaphore_wait(barrier, n * cols - 1)

    sends = []
    offsets = [n // 2]
    for i in range(1, n // 2):
        offsets += [n // 2 - i, n // 2 + i]

    def launch(copy):
        copy.start()
        sends.append(copy)

    def heads_send(t, source, target):
        for i in offsets:
            d = lax.rem(me + i, n)
            launch(remote(
                source.at[:, head_cols(d)], target.at[rows(me)],
                heads_s.at[t, i], heads_r.at[t, i], {"cp": d},
            ))

    def heads_arrival(t, i, target):
        source = lax.rem(me + n - i, n)
        block = target.at[rows(source)]
        remote(block, block, heads_s.at[t, i], heads_r.at[t, i], {"cp": source}).wait_recv()

    def heads_wait(t, target):
        for i in offsets:
            heads_arrival(t, i, target)

    def out_copy(t, i, source, target, place):
        d = lax.rem(me + i, n)
        return remote(
            source.at[rows(d)], target.at[:, cols_at(place)],
            out_s.at[t, i], out_r.at[t, i], {"cp": d},
        )

    def out_send(t, source, target, place):
        for i in offsets:
            launch(out_copy(t, i, source, target, place))

    def out_wait(t, target, place_of):
        for i in offsets:
            source = lax.rem(me + n - i, n)
            block = target.at[:, cols_at(place_of(source))]
            remote(block, block, out_s.at[t, i], out_r.at[t, i], {"cp": source}).wait_recv()

    def spot_of(d):
        return spot(lax.rem(d, 2), d // 2)

    def w_head(y, plane):
        return wall.at[rows_of(spot(y, plane) * HEAD, HEAD)]

    def w_pair(y, c):
        return wall.at[rows_of(spot(y, 2 * c) * HEAD, 2 * HEAD)]

    own_slab = rows_of(spot(why, zed) * HEAD + col * slab, slab)
    slab_copy = remote(
        w, wall.at[own_slab], slab_s.at[0], slab_r.at[col],
        {"fsdp": 2 * lax.rem(zed, 2) + zed // 2},
    )

    @pl.when(jnp.logical_not(root))
    def _():
        slab_copy.start()

    heads_send(0, k, kh)
    mine_up = ups.at[rows(2 * core + why)]
    launch(remote(up, mine_up, up_s.at[0], up_r.at[0], mate))
    launch(remote(up, mine_up, up_s.at[1], up_r.at[1], beside))

    gateway = jnp.logical_and(jnp.logical_not(keeper), zed == 1 + zed // 2)
    to_pair = jnp.logical_or(root, gateway)
    pair = 2 * (zed + 1 - 2 * lax.rem(zed, 2)) + why

    def piece_of(plane, p):
        return wall.at[rows_of(spot(why, plane) * HEAD + p * piece_rows, piece_rows)]

    def chain_copy(p, way):
        block = piece_of(home, p)
        target = pair if way == 0 else 2 * (2 - core) + why
        return remote(block, block, chain_s.at[way, p], chain_r.at[p], {"cp": target})

    def chain_forward(p):
        @pl.when(root)
        def _():
            chain_copy(p, 1).start()

        @pl.when(to_pair)
        def _():
            chain_copy(p, 0).start()

        block = piece_of(home, p)
        remote(block, block, side_s.at[p], side_r.at[p], across).start()

    @pl.when(root)
    def _():
        wall[own_slab] = w[...]
        for j in range(1, cols):
            other = lax.rem(col + j, cols)
            block = wall.at[rows_of(spot(why, zed) * HEAD + other * slab, slab)]
            remote(block, block, slab_s.at[0], slab_r.at[other], {"fsdp": other}).wait_recv()
        for p in range(pieces):
            chain_forward(p)

    heads_send(1, q, qh)
    for source, target in ((k, kh), (q, qh), (v, vh)):
        target[rows(me)] = source[:, head_cols(me)]
    ups[rows(2 * core + why)] = up[...]

    spans = order.shape[0]
    order_row = jnp.broadcast_to(order[...].reshape(1, spans), (spans, spans))
    place = lax.broadcasted_iota(jnp.int32, (spans, spans), 0)
    at_place = (order_row == place).astype(f32).astype(bf16)
    row = lax.broadcasted_iota(jnp.int32, (spans, length), 1)
    line = lax.broadcasted_iota(jnp.int32, (spans, length), 0)
    begin = line * span_rows
    member = jnp.logical_and(row >= begin, row < begin + span_rows).astype(f32)
    placed = jnp.dot(at_place, member.astype(bf16), preferred_element_type=f32)
    within = (row - begin).astype(f32) * member
    query_pos = (placed * begin.astype(f32) + within).sum(0, keepdims=True)
    key_pos = jnp.broadcast_to(query_pos, (8, length)).T[:, :1]
    placed_low = placed.astype(bf16)
    key_side = jnp.dot(
        mask[...].astype(f32).astype(bf16), placed_low, preferred_element_type=f32
    ).T.astype(bf16)
    for o in range(n):
        part = slice(o * tokens, (o + 1) * tokens)
        seen = jnp.dot(key_side, placed_low[:, part], preferred_element_type=f32)
        allowed = jnp.logical_and(seen > 0.5, key_pos <= query_pos[:, part])
        bias[:, part] = jnp.where(allowed, 0.0, lowest)

    def chain_relay(p):
        @pl.when(jnp.logical_not(root))
        def _():
            block = piece_of(home, p)
            remote(block, block, chain_s.at[0, p], chain_r.at[p], {"cp": me}).wait_recv()
            chain_forward(p)

    heads_wait(0, kh)
    heads_send(2, v, vh)
    kt[...] = kh[...].astype(f32).T.astype(bf16)
    for p in range(pieces // 2):
        chain_relay(p)
    beside_up = ups.at[rows(2 * core + 1 - why)]
    remote(beside_up, beside_up, up_s.at[1], up_r.at[1], beside).wait_recv()
    launch(remote(beside_up, beside_up, up_s.at[2], up_r.at[2], mate))
    for p in range(pieces // 2, pieces):
        chain_relay(p)

    for p in range(pieces):
        block = piece_of(2 * core + 1 - ex, p)
        remote(block, block, side_s.at[p], side_r.at[p], across).wait_recv()

    def seq_copy(ss, rs, slot, source, target, j, c):
        return remote(
            source, target, ss.at[slot], rs.at[zed], {"cp": 2 * (2 * core + j) + why, "fsdp": 2 * ex + c}
        )

    def seq_send(copy, here, j, i):
        if i:
            launch(copy)
            return
        stays = 2 * core + j == zed

        @pl.when(stays)
        def _():
            here()

        @pl.when(jnp.logical_not(stays))
        def _():
            copy.start()

    def seq_settle(copy, j):
        @pl.when(2 * core + j != zed)
        def _():
            copy.wait_send()

    def seq_wait(ss, rs, block_of):
        for i in range(planes):
            source = lax.rem(zed + i, planes)
            block = block_of(source)
            arrived = remote(block, block, ss.at[0], rs.at[source], {"cp": me})
            if i == 0:
                @pl.when(jnp.logical_not(keeper))
                def _():
                    arrived.wait_recv()
            else:
                arrived.wait_recv()

    def ga_copy(i, j):
        c = core if i == 0 else 1 - core
        return seq_copy(
            ga_s, ga_r, 2 * i + j,
            ga_out.at[j, two_rows(c)], ga.at[two_rows(zed)], j, c,
        )

    def ga_group(i):
        c = core if i == 0 else 1 - core
        weight = wall[rows_of(spot(why, 2 * core) * HEAD, 2 * HEAD)]
        result = lax.dot_general(
            ups[two_rows(c)], weight, nt, preferred_element_type=f32
        ).astype(bf16)
        for j in range(2):
            ga_out[j, two_rows(c)] = result[:, j * HEAD:(j + 1) * HEAD]

            def here(j=j):
                ga[two_rows(zed)] = result[:, j * HEAD:(j + 1) * HEAD]

            seq_send(ga_copy(i, j), here, j, i)

    ga_group(0)
    for slot, y in ((0, why), (2, 1 - why)):
        block = ups.at[rows(2 * (1 - core) + y)]
        remote(block, block, up_s.at[slot], up_r.at[slot], mate).wait_recv()
    ga_group(1)
    launch(remote(w_pair(why, core), w_pair(why, core), wide_s.at[0], wide_r.at[0], mate))
    launch(remote(w_head(why, home), w_head(why, home), wide_s.at[1], wide_r.at[1], beside))

    def soft(i, carry):
        @pl.when(i > 0)
        def _():
            heads_arrival(1, i, qh)

        part = rows(lax.rem(me + n - i, n))
        scores = lax.dot_general(kh[...], qh[part], nt, preferred_element_type=f32) * (1.0 / HEAD)
        scores = scores + bias[:, part]
        terms = jnp.exp(scores - scores.max(0, keepdims=True))
        probability = terms * (1.0 / terms.sum(0, keepdims=True))
        prob[:, part] = probability.astype(bf16)
        return carry

    lax.fori_loop(0, n, soft, 0)

    heads_wait(2, vh)
    vt[...] = vh[...].astype(f32).T.astype(bf16)

    def attend(o, carry):
        part = two_rows(o)
        att_t = jnp.dot(vt[...], prob[:, part], preferred_element_type=f32)
        att[part] = att_t.T.astype(bf16)
        return carry

    lax.fori_loop(0, n // 2, attend, 0)
    out_send(0, att, attended, spot_of(me))
    attended[:, cols_at(spot_of(me))] = att[rows(me)]
    seq_wait(ga_s, ga_r, lambda source: ga.at[two_rows(source)])

    def value_step(o, carry):
        part = two_rows(o)
        dvh[part] = jnp.dot(prob[part], ga[...], preferred_element_type=f32).astype(bf16)
        return carry

    lax.fori_loop(0, n // 2, value_step, 0)
    out_send(2, dvh, dv, me)
    dv[:, head_cols(me)] = dvh[rows(me)]

    block = w_head(1 - why, home)
    remote(block, block, wide_s.at[1], wide_r.at[1], beside).wait_recv()
    launch(remote(block, block, wide_s.at[2], wide_r.at[2], across))
    launch(remote(block, block, wide_s.at[3], wide_r.at[3], mate))

    def backward(i, carry):
        i = lax.rem(i + n // 2, n)
        o = lax.rem(me + i, n)
        part = rows(o)
        ga_rows = ga[part]
        delta = (att[part].astype(f32) * ga_rows.astype(f32)).T.sum(0, keepdims=True)
        dprob = lax.dot_general(vh[...], ga_rows, nt, preferred_element_type=f32)
        ds = (prob[:, part].astype(f32) * ((dprob - delta) * (1.0 / HEAD))).astype(bf16)
        dsb[:, part] = ds
        dqh[part] = jnp.dot(kt[...], ds, preferred_element_type=f32).T.astype(bf16)

        @pl.when(i > 0)
        def _():
            out_copy(3, i, dqh, dq, me).start()

        return carry

    lax.fori_loop(0, n, backward, 0)
    dq[:, head_cols(me)] = dqh[rows(me)]

    out_wait(0, attended, spot_of)
    for i in range(2):
        for j in range(2):
            y = why if i == 0 else 1 - why
            c = core if j == 0 else 1 - core
            part = rows_of(spot(y, 2 * c) * HEAD, 2 * HEAD)
            if i == 0 and j == 0:
                attp[rows(2 * core + why)] = attended[:, part]
                continue
            launch(remote(
                attended.at[:, part], attp.at[rows(2 * core + why)],
                attp_s.at[2 * i + j], attp_r.at[2 * i + j],
                {"cp": 2 * zed + y, "fsdp": 2 * ex + c},
            ))

    def key_step(o, carry):
        part = two_rows(o)
        dkh[part] = jnp.dot(dsb[part], qh[...], preferred_element_type=f32).astype(bf16)
        return carry

    lax.fori_loop(0, n // 2, key_step, 0)
    out_send(1, dkh, dk, me)
    dk[:, head_cols(me)] = dkh[rows(me)]

    for i in range(2):
        for j in range(2):
            if i == 0 and j == 0:
                continue
            y = why if i == 0 else 1 - why
            c = core if j == 0 else 1 - core
            block = attp.at[rows(2 * c + y)]
            remote(
                block, block, attp_s.at[2 * i + j], attp_r.at[2 * i + j], {"cp": me}
            ).wait_recv()
    att_t = attp[...].astype(f32).T.astype(bf16)
    width = math.gcd(proj.shape[1], 512)

    def weigh(i, carry):
        part = rows_of(i * width, width)
        dw[:, part] = jnp.dot(att_t, ups[:, part], preferred_element_type=f32).astype(bf16)
        return carry

    lax.fori_loop(0, proj.shape[1] // width, weigh, 0)
    share = 2 * slab

    def dw_rows(j, x):
        return rows_of(j * HEAD + x * share, share)

    for j in range(2):
        launch(remote(
            dw.at[dw_rows(j, 1 - ex)], dwx.at[j], dwx_s.at[j], dwx_r.at[j], across
        ))

    def dw_copy(i, j):
        c = core if i == 0 else 1 - core
        return seq_copy(
            dw_s, dw_r, 2 * i + j, dwz.at[j, rows_of(c * slab, slab)], dwr.at[zed], j, c
        )

    for j in range(2):
        remote(dwx.at[j], dwx.at[j], dwx_s.at[j], dwx_r.at[j], across).wait_recv()
        dwz[j] = (dw[dw_rows(j, ex)].astype(f32) + dwx[j].astype(f32)).astype(bf16)
        for i in range(2):
            def here(j=j):
                dwr[zed] = dwz[j, rows_of(core * slab, slab)]

            seq_send(dw_copy(i, j), here, j, i)

    block = w_head(1 - why, 2 * core + 1 - ex)
    remote(block, block, wide_s.at[2], wide_r.at[2], across).wait_recv()
    launch(remote(block, block, wide_s.at[4], wide_r.at[4], mate))
    for slot, block in (
        (0, w_pair(why, 1 - core)),
        (3, w_head(1 - why, 2 * (1 - core) + ex)),
        (4, w_head(1 - why, 2 * (1 - core) + 1 - ex)),
    ):
        remote(block, block, wide_s.at[slot], wide_r.at[slot], mate).wait_recv()

    def project(i, carry):
        part = rows_of(i * width, width)
        proj[:, part] = jnp.dot(
            attended[...], wall[:, part], preferred_element_type=f32
        ).astype(bf16)
        return carry

    lax.fori_loop(0, proj.shape[1] // width, project, 0)
    seq_wait(dw_s, dw_r, lambda source: dwr.at[source])
    total = dwr[0].astype(f32)
    for j in range(1, planes):
        total = total + dwr[j].astype(f32)
    wg[...] = total
    out_wait(2, dv, lambda d: d)
    out_wait(3, dq, lambda d: d)
    out_wait(1, dk, lambda d: d)
    for copy in sends:
        copy.wait_send()
    for i in offsets:
        out_copy(3, i, dqh, dq, me).wait_send()

    @pl.when(jnp.logical_not(root))
    def _():
        slab_copy.wait_send()

    for j in range(2):
        seq_settle(ga_copy(0, j), j)
        seq_settle(dw_copy(0, j), j)

    for p in range(pieces):
        block = piece_of(home, p)
        remote(block, block, side_s.at[p], side_r.at[p], across).wait_send()

        @pl.when(to_pair)
        def _():
            chain_copy(p, 0).wait_send()

        @pl.when(root)
        def _():
            chain_copy(p, 1).wait_send()


def deliver_kernel(*refs):
    count = len(refs) // 2
    copies = [
        pltpu.make_async_copy(refs[t], refs[count + t], refs[-1].at[t]) for t in range(count)
    ]
    for copy in copies:
        copy.start()
    for copy in copies:
        copy.wait()


def by_heads(query_states, key_states, value_states, span_order, block_mask, output_weight, upstream):
    n = lax.axis_size("cp")
    m = lax.axis_size("fsdp")
    tokens, width = query_states.shape[1:]
    length = tokens * n
    model = upstream.shape[2]
    slab = output_weight.shape[0]
    bf16, f32 = jnp.bfloat16, jnp.float32
    shape = jax.ShapeDtypeStruct
    vmem = pl.BlockSpec(memory_space=pltpu.VMEM)
    dma = pltpu.SemaphoreType.DMA
    planes = n // 2
    pieces = 4
    head_array = pltpu.VMEM((length, HEAD), bf16)
    square = pltpu.VMEM((length, length), bf16)
    projected, dq, dk, dv, weight_gradient = pl.pallas_call(
        lambda *refs: layer_kernel(n, *refs),
        out_shape=(shape((tokens, model), bf16),)
        + (shape((tokens, width), bf16),) * 3
        + (shape((slab, model), f32),),
        in_specs=[pl.BlockSpec(memory_space=pltpu.HBM)] * 7,
        out_specs=(vmem,) * 5,
        scratch_shapes=[
            pltpu.VMEM((tokens, width), bf16), pltpu.VMEM((tokens, width), bf16),
            pltpu.VMEM((tokens, width), bf16), pltpu.VMEM((tokens, model), bf16),
            pltpu.VMEM((slab, model), bf16), pltpu.VMEM(span_order.shape, jnp.int32),
            pltpu.VMEM(block_mask.shape, jnp.int32), dma((7,)),
            head_array, head_array, head_array,
            pltpu.VMEM((4 * tokens, model), bf16), pltpu.VMEM((width, model), bf16),
            pltpu.VMEM((length, length), f32), square, square,
            head_array, pltpu.VMEM((tokens, width), bf16),
            pltpu.VMEM((4 * tokens, 2 * HEAD), bf16), pltpu.VMEM((2, 4 * tokens, HEAD), bf16),
            head_array, head_array, head_array, head_array,
            pltpu.VMEM((2 * HEAD, model), bf16), pltpu.VMEM((2, 2 * slab, model), bf16),
            pltpu.VMEM((2, 2 * slab, model), bf16), pltpu.VMEM((planes, slab, model), bf16),
            pltpu.VMEM((HEAD, length), bf16), pltpu.VMEM((HEAD, length), bf16),
            dma((3, n)), dma((3, n)), dma((4, n)), dma((4, n)),
            dma((3,)), dma((3,)), dma((5,)), dma((5,)),
            dma((1,)), dma((m,)), dma((2, pieces)), dma((pieces,)), dma((pieces,)), dma((pieces,)),
            dma((4,)), dma((planes,)), dma((4,)), dma((4,)),
            dma((2,)), dma((2,)), dma((4,)), dma((planes,)),
        ],
        compiler_params=pltpu.CompilerParams(
            collective_id=0, has_side_effects=True, vmem_limit_bytes=48 << 20
        ),
        name="layer",
    )(
        *(
            pltpu.with_memory_space_constraint(a, pltpu.HBM)
            for a in (
                query_states[0], key_states[0], value_states[0], upstream[0], output_weight,
                span_order, block_mask,
            )
        ),
    )
    results = (projected, dq, dk, dv, weight_gradient)
    projected, dq, dk, dv, weight_gradient = pl.pallas_call(
        deliver_kernel,
        out_shape=tuple(shape(r.shape, r.dtype) for r in results),
        in_specs=[pl.BlockSpec(memory_space=pl.ANY)] * 5,
        out_specs=(pl.BlockSpec(memory_space=pl.ANY),) * 5,
        scratch_shapes=[dma((5,))],
        compiler_params=pltpu.CompilerParams(vmem_limit_bytes=1 << 20),
        name="deliver",
    )(*results)
    return (projected[None], dq[None], dk[None], dv[None], weight_gradient)


def solution(mesh):
    fits = mesh.shape["cp"] == HEADS and mesh.shape["fsdp"] == 4
    return jax.shard_map(
        by_heads if fits else local,
        mesh=mesh,
        in_specs=(
            P("fsdp", "cp", None),
            P("fsdp", "cp", None),
            P("fsdp", "cp", None),
            P(),
            P(),
            P(("cp", "fsdp"), None),
            P("fsdp", "cp", None),
        ),
        out_specs=(
            P("fsdp", "cp", None),
            P("fsdp", "cp", None),
            P("fsdp", "cp", None),
            P("fsdp", "cp", None),
            P(("cp", "fsdp"), None),
        ),
        check_vma=False,
    )
```

time: 96.8 us -> 86.3 us (0.89)
  the two profiles are of different devices: /device:TPU:7 before, /device:TPU:11 now
where the time goes in v2:
time: 86.3 us; the launch traced here: 86.2 us
  Pallas kernels  85.5 us (99%)
    pallas_call x1, Pallas kernels, by_heads(): pl.pallas_call(lambda *refs: layer_kernel(n, *refs), out_shape=(shape((to...  84.4 us

profile of v2, /device:TPU:11, one launch (start us, length us, event | category | flops | bytes accessed | tf_op | source)
XLA Modules:
  0.0 86.2 jit_solution(12951608305924439428)
XLA Ops:
  0.6 84.4 %layer.1 = (bf16[128,2048]{1,0:T(8,128)(2,1)S(1)}, bf16[128,1024]{1,0:T(8,128)(2,1)S(1)}, bf16[128,1024]{1,0:T(8,128)(2,1)S(1)}, bf16[128,1024]{1,0:T(8,128)(2,1)S(1)}, f32[32,2048]{1,0:T(8,128)S(1)}) custom-call(bf16[128,1024]{1,0:T(8,128)(2,1)} %bitcast.9, bf16[128,1024]{1,0:T(8,128)(2,1)} %bitcast.10, bf16[128,1024]{1,0:T(8,128)(2,1)} %bitcast.11, ...), custom_call_target="tpu_custom_call" | custom-call | tf_op jit(solution)/shard_map/layer/pallas_call | solution.py:751
  85.0 1.2 %deliver.1 = (bf16[128,2048]{1,0:T(8,128)(2,1)}, bf16[128,1024]{1,0:T(8,128)(2,1)}, bf16[128,1024]{1,0:T(8,128)(2,1)}, bf16[128,1024]{1,0:T(8,128)(2,1)}, f32[32,2048]{1,0:T(8,128)}) custom-call(bf16[128,2048]{1,0:T(8,128)(2,1)S(1)} %get-tuple-element.15.refs_0_, bf16[128,1024]{1,0:T(8,128)(2,1)S(1)} %get-tuple-element.16.refs_1_, ...), custom_call_target="tpu_custom_call" | custom-call | tf_op jit(solution)/shard_map/deliver/pallas_call | solution.py:792

commit v3 on v2

--- a/solution.py
+++ b/solution.py
@@ -263,11 +263,11 @@
 def layer_kernel(
     n, q_in, k_in, v_in, up_in, w_in, order_in, mask_in, proj, dq, dk, dv, wg,
     q, k, v, up, w, order, mask, load,
-    qh, kh, vh, ups, wall, bias, prob, dsb, att, attended, attp, ga_out, ga,
-    dqh, dkh, dvh, dw, dwx, dwz, dwr, kt, vt,
-    heads_s, heads_r, out_s, out_r, up_s, up_r, wide_s, wide_r,
-    slab_s, slab_r, chain_s, chain_r, side_s, side_r, ga_s, ga_r, attp_s, attp_r,
-    dwx_s, dwx_r, dw_s, dw_r,
+    qh, kh, vh, ups, wall, bias, prob, dsb, att, attp, ga_out, ga,
+    dqh, dkh, dvh, dw, dwx, dwz, dwp, dwr, kt, vt, mix, mix_mate, mix_send, mix_beside,
+    heads_s, heads_r, out_s, out_r, up_s, up_r,
+    slab_s, slab_r, pass_s, side_s, side_r, ga_s, ga_r, att_s, att_r,
+    dwx_s, dwx_r, lift_s, lift_r, dw_s, dw_r, mix_s, mix_r,
 ):
     me = lax.axis_index("cp")
     col = lax.axis_index("fsdp")
@@ -287,14 +287,8 @@
     home = 2 * core + ex
     root = home == zed
     keeper = core == zed // 2
-    pieces = chain_r.shape[0]
-    piece_rows = HEAD // pieces
-
-    def spot(y, plane):
-        return y * planes + plane
-
-    def cols_at(place):
-        return rows_of(place * HEAD, HEAD)
+    gateway = jnp.logical_and(jnp.logical_not(keeper), zed == 1 + zed // 2)
+    pair = 2 * (zed + 1 - 2 * lax.rem(zed, 2)) + why
 
     def head_cols(d):
         return rows_of(d * HEAD, HEAD)
@@ -350,82 +344,71 @@
         for i in offsets:
             heads_arrival(t, i, target)
 
-    def out_copy(t, i, source, target, place):
+    def out_copy(t, i, source, target):
         d = lax.rem(me + i, n)
         return remote(
-            source.at[rows(d)], target.at[:, cols_at(place)],
+            source.at[rows(d)], target.at[:, head_cols(me)],
             out_s.at[t, i], out_r.at[t, i], {"cp": d},
         )
 
-    def out_send(t, source, target, place):
+    def out_send(t, source, target):
         for i in offsets:
-            launch(out_copy(t, i, source, target, place))
-
-    def out_wait(t, target, place_of):
+            launch(out_copy(t, i, source, target))
+
+    def out_wait(t, target):
         for i in offsets:
             source = lax.rem(me + n - i, n)
-            block = target.at[:, cols_at(place_of(source))]
+            block = target.at[:, head_cols(source)]
             remote(block, block, out_s.at[t, i], out_r.at[t, i], {"cp": source}).wait_recv()
 
-    def spot_of(d):
-        return spot(lax.rem(d, 2), d // 2)
-
-    def w_head(y, plane):
-        return wall.at[rows_of(spot(y, plane) * HEAD, HEAD)]
-
-    def w_pair(y, c):
-        return wall.at[rows_of(spot(y, 2 * c) * HEAD, 2 * HEAD)]
-
-    own_slab = rows_of(spot(why, zed) * HEAD + col * slab, slab)
-    slab_copy = remote(
-        w, wall.at[own_slab], slab_s.at[0], slab_r.at[col],
-        {"fsdp": 2 * lax.rem(zed, 2) + zed // 2},
-    )
+    own_slab = rows_of(lax.rem(zed, 2) * HEAD + col * slab, slab)
+    slab_copies = [
+        remote(
+            w, wall.at[own_slab], slab_s.at[i], slab_r.at[col],
+            {"cp": target, "fsdp": 2 * lax.rem(zed, 2) + zed // 2},
+        )
+        for i, target in enumerate((me, pair, 2 * (2 - zed // 2) + why))
+    ]
+    launch(slab_copies[2])
 
     @pl.when(jnp.logical_not(root))
     def _():
-        slab_copy.start()
-
+        slab_copies[0].start()
+
+    launch(slab_copies[1])
+    mine_up = ups.at[rows(2 * core + why)]
+    launch(remote(up, mine_up, up_s.at[1], up_r.at[1], beside))
     heads_send(0, k, kh)
-    mine_up = ups.at[rows(2 * core + why)]
     launch(remote(up, mine_up, up_s.at[0], up_r.at[0], mate))
-    launch(remote(up, mine_up, up_s.at[1], up_r.at[1], beside))
-
-    gateway = jnp.logical_and(jnp.logical_not(keeper), zed == 1 + zed // 2)
-    to_pair = jnp.logical_or(root, gateway)
-    pair = 2 * (zed + 1 - 2 * lax.rem(zed, 2)) + why
+    heads_send(1, q, qh)
+
+    @pl.when(root)
+    def _():
+        wall[own_slab] = w[...]
 
     def piece_of(plane, p):
-        return wall.at[rows_of(spot(why, plane) * HEAD + p * piece_rows, piece_rows)]
-
-    def chain_copy(p, way):
+        return wall.at[rows_of(lax.rem(plane, 2) * HEAD + p * slab, slab)]
+
+    def pass_copy(p):
         block = piece_of(home, p)
-        target = pair if way == 0 else 2 * (2 - core) + why
-        return remote(block, block, chain_s.at[way, p], chain_r.at[p], {"cp": target})
-
-    def chain_forward(p):
-        @pl.when(root)
-        def _():
-            chain_copy(p, 1).start()
-
-        @pl.when(to_pair)
-        def _():
-            chain_copy(p, 0).start()
-
+        return remote(block, block, pass_s.at[p], slab_r.at[p], {"cp": pair})
+
+    def side_copy(p):
         block = piece_of(home, p)
-        remote(block, block, side_s.at[p], side_r.at[p], across).start()
-
-    @pl.when(root)
-    def _():
-        wall[own_slab] = w[...]
-        for j in range(1, cols):
-            other = lax.rem(col + j, cols)
-            block = wall.at[rows_of(spot(why, zed) * HEAD + other * slab, slab)]
-            remote(block, block, slab_s.at[0], slab_r.at[other], {"fsdp": other}).wait_recv()
-        for p in range(pieces):
-            chain_forward(p)
-
-    heads_send(1, q, qh)
+        return remote(block, block, side_s.at[p], side_r.at[p], across)
+
+    def piece_poll(p):
+        @pl.when(jnp.logical_not(jnp.logical_and(root, col == p)))
+        def _():
+            block = piece_of(home, p)
+            remote(block, block, slab_s.at[0], slab_r.at[p], mate).wait_recv()
+
+        @pl.when(gateway)
+        def _():
+            pass_copy(p).start()
+
+        side_copy(p).start()
+
     for source, target in ((k, kh), (q, qh), (v, vh)):
         target[rows(me)] = source[:, head_cols(me)]
     ups[rows(2 * core + why)] = up[...]
@@ -452,27 +435,38 @@
         allowed = jnp.logical_and(seen > 0.5, key_pos <= query_pos[:, part])
         bias[:, part] = jnp.where(allowed, 0.0, lowest)
 
-    def chain_relay(p):
-        @pl.when(jnp.logical_not(root))
-        def _():
-            block = piece_of(home, p)
-            remote(block, block, chain_s.at[0, p], chain_r.at[p], {"cp": me}).wait_recv()
-            chain_forward(p)
-
+    far = jnp.logical_not(jnp.logical_or(keeper, gateway))
+
+    @pl.when(jnp.logical_not(far))
+    def _():
+        for p in range(cols):
+            piece_poll(p)
+
+    heads_send(2, v, vh)
     heads_wait(0, kh)
-    heads_send(2, v, vh)
     kt[...] = kh[...].astype(f32).T.astype(bf16)
-    for p in range(pieces // 2):
-        chain_relay(p)
     beside_up = ups.at[rows(2 * core + 1 - why)]
     remote(beside_up, beside_up, up_s.at[1], up_r.at[1], beside).wait_recv()
     launch(remote(beside_up, beside_up, up_s.at[2], up_r.at[2], mate))
-    for p in range(pieces // 2, pieces):
-        chain_relay(p)
-
-    for p in range(pieces):
-        block = piece_of(2 * core + 1 - ex, p)
-        remote(block, block, side_s.at[p], side_r.at[p], across).wait_recv()
+    @pl.when(far)
+    def _():
+        for p in range(cols // 2):
+            piece_poll(p)
+
+    def soft(i, carry):
+        @pl.when(i > 0)
+        def _():
+            heads_arrival(1, i, qh)
+
+        part = rows(lax.rem(me + n - i, n))
+        scores = lax.dot_general(kh[...], qh[part], nt, preferred_element_type=f32) * (1.0 / HEAD)
+        scores = scores + bias[:, part]
+        terms = jnp.exp(scores - scores.max(0, keepdims=True))
+        probability = terms * (1.0 / terms.sum(0, keepdims=True))
+        prob[:, part] = probability.astype(bf16)
+        return carry
+
+    lax.fori_loop(0, n, soft, 0)
 
     def seq_copy(ss, rs, slot, source, target, j, c):
         return remote(
@@ -481,7 +475,7 @@
 
     def seq_send(copy, here, j, i):
         if i:
-            launch(copy)
+            copy.start()
             return
         stays = 2 * core + j == zed
 
@@ -519,9 +513,8 @@
 
     def ga_group(i):
         c = core if i == 0 else 1 - core
-        weight = wall[rows_of(spot(why, 2 * core) * HEAD, 2 * HEAD)]
         result = lax.dot_general(
-            ups[two_rows(c)], weight, nt, preferred_element_type=f32
+            ups[two_rows(c)], wall[...], nt, preferred_element_type=f32
         ).astype(bf16)
         for j in range(2):
             ga_out[j, two_rows(c)] = result[:, j * HEAD:(j + 1) * HEAD]
@@ -531,28 +524,25 @@
 
             seq_send(ga_copy(i, j), here, j, i)
 
-    ga_group(0)
-    for slot, y in ((0, why), (2, 1 - why)):
-        block = ups.at[rows(2 * (1 - core) + y)]
-        remote(block, block, up_s.at[slot], up_r.at[slot], mate).wait_recv()
-    ga_group(1)
-    launch(remote(w_pair(why, core), w_pair(why, core), wide_s.at[0], wide_r.at[0], mate))
-    launch(remote(w_head(why, home), w_head(why, home), wide_s.at[1], wide_r.at[1], beside))
-
-    def soft(i, carry):
-        @pl.when(i > 0)
-        def _():
-            heads_arrival(1, i, qh)
-
-        part = rows(lax.rem(me + n - i, n))
-        scores = lax.dot_general(kh[...], qh[part], nt, preferred_element_type=f32) * (1.0 / HEAD)
-        scores = scores + bias[:, part]
-        terms = jnp.exp(scores - scores.max(0, keepdims=True))
-        probability = terms * (1.0 / terms.sum(0, keepdims=True))
-        prob[:, part] = probability.astype(bf16)
-        return carry
-
-    lax.fori_loop(0, n, soft, 0)
+    def work_gradient():
+        for p in range(cols):
+            block = piece_of(2 * core + 1 - ex, p)
+            remote(block, block, side_s.at[p], side_r.at[p], across).wait_recv()
+
+        ga_group(0)
+        for slot, y in ((0, why), (2, 1 - why)):
+            block = ups.at[rows(2 * (1 - core) + y)]
+            remote(block, block, up_s.at[slot], up_r.at[slot], mate).wait_recv()
+        ga_group(1)
+
+    @pl.when(far)
+    def _():
+        for p in range(cols // 2, cols):
+            piece_poll(p)
+
+    @pl.when(jnp.logical_not(far))
+    def _():
+        work_gradient()
 
     heads_wait(2, vh)
     vt[...] = vh[...].astype(f32).T.astype(bf16)
@@ -564,8 +554,72 @@
         return carry
 
     lax.fori_loop(0, n // 2, attend, 0)
-    out_send(0, att, attended, spot_of(me))
-    attended[:, cols_at(spot_of(me))] = att[rows(me)]
+
+    def att_copy(i):
+        plane = lax.rem(zed + i, planes)
+        return remote(
+            att.at[two_rows(plane)], attp.at[lax.rem(zed, 2), two_rows(core)],
+            att_s.at[i], att_r.at[2 * lax.rem(zed, 2) + core],
+            {"cp": 2 * plane + why, "fsdp": 2 * ex + zed // 2},
+        )
+
+    for i in (2, 1, 3):
+        launch(att_copy(i))
+
+    @pl.when(keeper)
+    def _():
+        attp[lax.rem(zed, 2), two_rows(core)] = att[two_rows(zed)]
+
+    @pl.when(jnp.logical_not(keeper))
+    def _():
+        att_copy(0).start()
+
+    @pl.when(far)
+    def _():
+        work_gradient()
+
+    width = math.gcd(proj.shape[1], 512)
+
+    for j in range(2):
+        for c in range(2):
+            block = attp.at[j, 2 * c * tokens:2 * (c + 1) * tokens]
+            arrived = remote(block, block, att_s.at[0], att_r.at[2 * j + c], {"cp": me})
+
+            @pl.when(jnp.logical_not(jnp.logical_and(2 * core + j == zed, core == c)))
+            def _():
+                arrived.wait_recv()
+
+    att_t = jnp.concatenate(
+        [attp[0].astype(f32).T.astype(bf16), attp[1].astype(f32).T.astype(bf16)], axis=0
+    )
+    att_both = jnp.concatenate([attp[0], attp[1]], axis=1)
+
+    def weigh(i, carry):
+        lanes = rows_of(i * width, width)
+        dw[:, lanes] = jnp.dot(att_t, ups[:, lanes], preferred_element_type=f32).astype(bf16)
+        return carry
+
+    def project(i, carry):
+        lanes = rows_of(i * width, width)
+        mix[:, lanes] = jnp.dot(
+            att_both, wall[:, lanes], preferred_element_type=f32
+        ).astype(bf16)
+        return carry
+
+    lax.fori_loop(0, proj.shape[1] // width, weigh, 0)
+    share = 2 * slab
+
+    def dw_rows(j, x):
+        return rows_of(j * HEAD + x * share, share)
+
+    for j in range(2):
+        launch(remote(
+            dw.at[dw_rows(j, 1 - ex)], dwx.at[j], dwx_s.at[j], dwx_r.at[j], across
+        ))
+
+    lax.fori_loop(0, proj.shape[1] // width, project, 0)
+    launch(remote(mix.at[two_rows(1 - core)], mix_mate, mix_s.at[0], mix_r.at[0], mate))
+
     seq_wait(ga_s, ga_r, lambda source: ga.at[two_rows(source)])
 
     def value_step(o, carry):
@@ -574,13 +628,15 @@
         return carry
 
     lax.fori_loop(0, n // 2, value_step, 0)
-    out_send(2, dvh, dv, me)
+    out_send(2, dvh, dv)
     dv[:, head_cols(me)] = dvh[rows(me)]
 
-    block = w_head(1 - why, home)
-    remote(block, block, wide_s.at[1], wide_r.at[1], beside).wait_recv()
-    launch(remote(block, block, wide_s.at[2], wide_r.at[2], across))
-    launch(remote(block, block, wide_s.at[3], wide_r.at[3], mate))
+    remote(mix_mate, mix_mate, mix_s.at[0], mix_r.at[0], mate).wait_recv()
+    theirs, ours = rows(1 - why), rows(why)
+    mix_send[...] = (
+        mix[rows(2 * core + 1 - why)].astype(f32) + mix_mate[theirs].astype(f32)
+    ).astype(bf16)
+    launch(remote(mix_send, mix_beside, mix_s.at[1], mix_r.at[1], beside))
 
     def backward(i, carry):
         i = lax.rem(i + n // 2, n)
@@ -595,27 +651,46 @@
 
         @pl.when(i > 0)
         def _():
-            out_copy(3, i, dqh, dq, me).start()
+            out_copy(0, i, dqh, dq).start()
 
         return carry
 
     lax.fori_loop(0, n, backward, 0)
     dq[:, head_cols(me)] = dqh[rows(me)]
 
-    out_wait(0, attended, spot_of)
-    for i in range(2):
-        for j in range(2):
-            y = why if i == 0 else 1 - why
-            c = core if j == 0 else 1 - core
-            part = rows_of(spot(y, 2 * c) * HEAD, 2 * HEAD)
-            if i == 0 and j == 0:
-                attp[rows(2 * core + why)] = attended[:, part]
-                continue
-            launch(remote(
-                attended.at[:, part], attp.at[rows(2 * core + why)],
-                attp_s.at[2 * i + j], attp_r.at[2 * i + j],
-                {"cp": 2 * zed + y, "fsdp": 2 * ex + c},
-            ))
+    outer = jnp.logical_not(jnp.logical_or(keeper, gateway))
+
+    def dw_copy(i, j):
+        c = core if i == 0 else 1 - core
+        return remote(
+            dwz.at[j, rows_of(c * slab, slab)],
+            dwr.at[jnp.where(keeper, jnp.where(2 * core + j == zed, 0, 1), 2)],
+            dw_s.at[2 * i + j],
+            dw_r.at[jnp.where(keeper, jnp.where(2 * core + j == zed, 0, 1), 2)],
+            {"cp": 2 * (2 * core + j) + why, "fsdp": 2 * ex + c},
+        )
+
+    def lift_copy(j):
+        return remote(dwz.at[j], dwp.at[j], lift_s.at[j], lift_r.at[j], {"cp": pair})
+
+    def dw_send(j):
+        for i in range(2):
+            def here(j=j):
+                dwr[0] = dwz[j, rows_of(core * slab, slab)]
+
+            seq_send(dw_copy(i, j), here, j, i)
+
+    for j in range(2):
+        remote(dwx.at[j], dwx.at[j], dwx_s.at[j], dwx_r.at[j], across).wait_recv()
+        dwz[j] = (dw[dw_rows(j, ex)].astype(f32) + dwx[j].astype(f32)).astype(bf16)
+
+        @pl.when(outer)
+        def _():
+            lift_copy(j).start()
+
+        @pl.when(keeper)
+        def _():
+            dw_send(j)
 
     def key_step(o, carry):
         part = two_rows(o)
@@ -623,103 +698,69 @@
         return carry
 
     lax.fori_loop(0, n // 2, key_step, 0)
-    out_send(1, dkh, dk, me)
+    out_send(1, dkh, dk)
     dk[:, head_cols(me)] = dkh[rows(me)]
 
-    for i in range(2):
+    @pl.when(gateway)
+    def _():
         for j in range(2):
-            if i == 0 and j == 0:
-                continue
-            y = why if i == 0 else 1 - why
-            c = core if j == 0 else 1 - core
-            block = attp.at[rows(2 * c + y)]
-            remote(
-                block, block, attp_s.at[2 * i + j], attp_r.at[2 * i + j], {"cp": me}
-            ).wait_recv()
-    att_t = attp[...].astype(f32).T.astype(bf16)
-    width = math.gcd(proj.shape[1], 512)
-
-    def weigh(i, carry):
-        part = rows_of(i * width, width)
-        dw[:, part] = jnp.dot(att_t, ups[:, part], preferred_element_type=f32).astype(bf16)
-        return carry
-
-    lax.fori_loop(0, proj.shape[1] // width, weigh, 0)
-    share = 2 * slab
-
-    def dw_rows(j, x):
-        return rows_of(j * HEAD + x * share, share)
-
-    for j in range(2):
-        launch(remote(
-            dw.at[dw_rows(j, 1 - ex)], dwx.at[j], dwx_s.at[j], dwx_r.at[j], across
-        ))
-
-    def dw_copy(i, j):
-        c = core if i == 0 else 1 - core
-        return seq_copy(
-            dw_s, dw_r, 2 * i + j, dwz.at[j, rows_of(c * slab, slab)], dwr.at[zed], j, c
-        )
-
-    for j in range(2):
-        remote(dwx.at[j], dwx.at[j], dwx_s.at[j], dwx_r.at[j], across).wait_recv()
-        dwz[j] = (dw[dw_rows(j, ex)].astype(f32) + dwx[j].astype(f32)).astype(bf16)
-        for i in range(2):
-            def here(j=j):
-                dwr[zed] = dwz[j, rows_of(core * slab, slab)]
-
-            seq_send(dw_copy(i, j), here, j, i)
-
-    block = w_head(1 - why, 2 * core + 1 - ex)
-    remote(block, block, wide_s.at[2], wide_r.at[2], across).wait_recv()
-    launch(remote(block, block, wide_s.at[4], wide_r.at[4], mate))
-    for slot, block in (
-        (0, w_pair(why, 1 - core)),
-        (3, w_head(1 - why, 2 * (1 - core) + ex)),
-        (4, w_head(1 - why, 2 * (1 - core) + 1 - ex)),
-    ):
-        remote(block, block, wide_s.at[slot], wide_r.at[slot], mate).wait_recv()
-
-    def project(i, carry):
-        part = rows_of(i * width, width)
-        proj[:, part] = jnp.dot(
-            attended[...], wall[:, part], preferred_element_type=f32
-        ).astype(bf16)
-        return carry
-
-    lax.fori_loop(0, proj.shape[1] // width, project, 0)
-    seq_wait(dw_s, dw_r, lambda source: dwr.at[source])
-    total = dwr[0].astype(f32)
-    for j in range(1, planes):
-        total = total + dwr[j].astype(f32)
+            lift_copy(j).wait_recv()
+            dwz[j] = (dwz[j].astype(f32) + dwp[j].astype(f32)).astype(bf16)
+            dw_send(j)
+
+    remote(mix_beside, mix_beside, mix_s.at[1], mix_r.at[1], beside).wait_recv()
+    proj[...] = (
+        mix[rows(2 * core + why)].astype(f32) + mix_mate[ours].astype(f32)
+        + mix_beside[...].astype(f32)
+    ).astype(bf16)
+    for t in range(3):
+        arrived = remote(dwr.at[t], dwr.at[t], dw_s.at[0], dw_r.at[t], {"cp": me})
+        if t == 0:
+            @pl.when(jnp.logical_not(keeper))
+            def _():
+                arrived.wait_recv()
+        else:
+            arrived.wait_recv()
+    total = dwr[0].astype(f32) + dwr[1].astype(f32) + dwr[2].astype(f32)
     wg[...] = total
-    out_wait(2, dv, lambda d: d)
-    out_wait(3, dq, lambda d: d)
-    out_wait(1, dk, lambda d: d)
+    out_wait(2, dv)
+    out_wait(0, dq)
+    out_wait(1, dk)
     for copy in sends:
         copy.wait_send()
     for i in offsets:
-        out_copy(3, i, dqh, dq, me).wait_send()
+        out_copy(0, i, dqh, dq).wait_send()
 
     @pl.when(jnp.logical_not(root))
     def _():
-        slab_copy.wait_send()
+        slab_copies[0].wait_send()
+
+    @pl.when(jnp.logical_not(keeper))
+    def _():
+        att_copy(0).wait_send()
 
     for j in range(2):
         seq_settle(ga_copy(0, j), j)
-        seq_settle(dw_copy(0, j), j)
-
-    for p in range(pieces):
-        block = piece_of(home, p)
-        remote(block, block, side_s.at[p], side_r.at[p], across).wait_send()
-
-        @pl.when(to_pair)
-        def _():
-            chain_copy(p, 0).wait_send()
-
-        @pl.when(root)
-        def _():
-            chain_copy(p, 1).wait_send()
+        ga_copy(1, j).wait_send()
+
+    for p in range(cols):
+        side_copy(p).wait_send()
+
+    for j in range(2):
+        @pl.when(outer)
+        def _():
+            lift_copy(j).wait_send()
+
+        @pl.when(jnp.logical_not(outer))
+        def _():
+            seq_settle(dw_copy(0, j), j)
+            dw_copy(1, j).wait_send()
+
+
+    @pl.when(gateway)
+    def _():
+        for p in range(cols):
+            pass_copy(p).wait_send()
 
 
 def deliver_kernel(*refs):
@@ -745,7 +786,6 @@
     vmem = pl.BlockSpec(memory_space=pltpu.VMEM)
     dma = pltpu.SemaphoreType.DMA
     planes = n // 2
-    pieces = 4
     head_array = pltpu.VMEM((length, HEAD), bf16)
     square = pltpu.VMEM((length, length), bf16)
     projected, dq, dk, dv, weight_gradient = pl.pallas_call(
@@ -761,19 +801,21 @@
             pltpu.VMEM((slab, model), bf16), pltpu.VMEM(span_order.shape, jnp.int32),
             pltpu.VMEM(block_mask.shape, jnp.int32), dma((7,)),
             head_array, head_array, head_array,
-            pltpu.VMEM((4 * tokens, model), bf16), pltpu.VMEM((width, model), bf16),
+            pltpu.VMEM((4 * tokens, model), bf16), pltpu.VMEM((2 * HEAD, model), bf16),
             pltpu.VMEM((length, length), f32), square, square,
-            head_array, pltpu.VMEM((tokens, width), bf16),
-            pltpu.VMEM((4 * tokens, 2 * HEAD), bf16), pltpu.VMEM((2, 4 * tokens, HEAD), bf16),
+            head_array, pltpu.VMEM((2, 4 * tokens, HEAD), bf16),
+            pltpu.VMEM((2, 4 * tokens, HEAD), bf16),
             head_array, head_array, head_array, head_array,
             pltpu.VMEM((2 * HEAD, model), bf16), pltpu.VMEM((2, 2 * slab, model), bf16),
-            pltpu.VMEM((2, 2 * slab, model), bf16), pltpu.VMEM((planes, slab, model), bf16),
+            pltpu.VMEM((2, 2 * slab, model), bf16),
+            pltpu.VMEM((2, 2 * slab, model), bf16), pltpu.VMEM((3, slab, model), bf16),
             pltpu.VMEM((HEAD, length), bf16), pltpu.VMEM((HEAD, length), bf16),
-            dma((3, n)), dma((3, n)), dma((4, n)), dma((4, n)),
-            dma((3,)), dma((3,)), dma((5,)), dma((5,)),
-            dma((1,)), dma((m,)), dma((2, pieces)), dma((pieces,)), dma((pieces,)), dma((pieces,)),
-            dma((4,)), dma((planes,)), dma((4,)), dma((4,)),
-            dma((2,)), dma((2,)), dma((4,)), dma((planes,)),
+            pltpu.VMEM((4 * tokens, model), bf16), pltpu.VMEM((2 * tokens, model), bf16),
+            pltpu.VMEM((tokens, model), bf16), pltpu.VMEM((tokens, model), bf16),
+            dma((3, n)), dma((3, n)), dma((3, n)), dma((3, n)), dma((3,)), dma((3,)),
+            dma((3,)), dma((m,)), dma((m,)), dma((m,)), dma((m,)),
+            dma((4,)), dma((planes,)), dma((planes,)), dma((4,)),
+            dma((2,)), dma((2,)), dma((2,)), dma((2,)), dma((4,)), dma((3,)), dma((2,)), dma((2,)),
         ],
         compiler_params=pltpu.CompilerParams(
             collective_id=0, has_side_effects=True, vmem_limit_bytes=48 << 20

time: 86.3 us -> 75.5 us (0.87); the launches traced: 86.2 us -> 74.3 us
  Pallas kernels: 85.5 us -> 73.7 us
    pallas_call x1, Pallas kernels: 84.4 us -> 72.5 us  [by_heads(): pl.pallas_call(lambda *refs: layer_kernel(n, *refs), out_shape=(shape((to...]
where the time goes in v3:
time: 75.5 us; the launch traced here: 74.3 us
  Pallas kernels  73.7 us (98%)
    pallas_call x1, Pallas kernels, by_heads(): pl.pallas_call(lambda *refs: layer_kernel(n, *refs), out_shape=(shape((to...  72.5 us

profile of v3, /device:TPU:11, one launch (start us, length us, event | category | flops | bytes accessed | tf_op | source)
XLA Modules:
  0.0 74.3 jit_solution(15391806408737624987)
XLA Ops:
  0.6 72.5 %layer.1 = (bf16[128,2048]{1,0:T(8,128)(2,1)S(1)}, bf16[128,1024]{1,0:T(8,128)(2,1)S(1)}, bf16[128,1024]{1,0:T(8,128)(2,1)S(1)}, bf16[128,1024]{1,0:T(8,128)(2,1)S(1)}, f32[32,2048]{1,0:T(8,128)S(1)}) custom-call(bf16[128,1024]{1,0:T(8,128)(2,1)} %bitcast.9, bf16[128,1024]{1,0:T(8,128)(2,1)} %bitcast.10, bf16[128,1024]{1,0:T(8,128)(2,1)} %bitcast.11, ...), custom_call_target="tpu_custom_call" | custom-call | tf_op jit(solution)/shard_map/layer/pallas_call | solution.py:791
  73.1 1.2 %deliver.1 = (bf16[128,2048]{1,0:T(8,128)(2,1)}, bf16[128,1024]{1,0:T(8,128)(2,1)}, bf16[128,1024]{1,0:T(8,128)(2,1)}, bf16[128,1024]{1,0:T(8,128)(2,1)}, f32[32,2048]{1,0:T(8,128)}) custom-call(bf16[128,2048]{1,0:T(8,128)(2,1)S(1)} %get-tuple-element.15.refs_0_, bf16[128,1024]{1,0:T(8,128)(2,1)S(1)} %get-tuple-element.16.refs_1_, ...), custom_call_target="tpu_custom_call" | custom-call | tf_op jit(solution)/shard_map/deliver/pallas_call | solution.py:834

commit v4 on v3

--- a/solution.py
+++ b/solution.py
@@ -442,8 +442,8 @@
         for p in range(cols):
             piece_poll(p)
 
+    heads_wait(0, kh)
     heads_send(2, v, vh)
-    heads_wait(0, kh)
     kt[...] = kh[...].astype(f32).T.astype(bf16)
     beside_up = ups.at[rows(2 * core + 1 - why)]
     remote(beside_up, beside_up, up_s.at[1], up_r.at[1], beside).wait_recv()
@@ -631,13 +631,6 @@
     out_send(2, dvh, dv)
     dv[:, head_cols(me)] = dvh[rows(me)]
 
-    remote(mix_mate, mix_mate, mix_s.at[0], mix_r.at[0], mate).wait_recv()
-    theirs, ours = rows(1 - why), rows(why)
-    mix_send[...] = (
-        mix[rows(2 * core + 1 - why)].astype(f32) + mix_mate[theirs].astype(f32)
-    ).astype(bf16)
-    launch(remote(mix_send, mix_beside, mix_s.at[1], mix_r.at[1], beside))
-
     def backward(i, carry):
         i = lax.rem(i + n // 2, n)
         o = lax.rem(me + i, n)
@@ -655,7 +648,15 @@
 
         return carry
 
-    lax.fori_loop(0, n, backward, 0)
+    lax.fori_loop(0, n // 2, backward, 0)
+    remote(mix_mate, mix_mate, mix_s.at[0], mix_r.at[0], mate).wait_recv()
+    theirs, ours = rows(1 - why), rows(why)
+    mix_send[...] = (
+        mix[rows(2 * core + 1 - why)].astype(f32) + mix_mate[theirs].astype(f32)
+    ).astype(bf16)
+    launch(remote(mix_send, mix_beside, mix_s.at[1], mix_r.at[1], beside))
+
+    lax.fori_loop(n // 2, n, backward, 0)
     dq[:, head_cols(me)] = dqh[rows(me)]
 
     outer = jnp.logical_not(jnp.logical_or(keeper, gateway))

time: 75.5 us -> 72.6 us (0.962)
  Pallas kernels: 73.7 us -> 71.1 us
    pallas_call x1, Pallas kernels: 72.5 us -> 69.9 us  [by_heads(): pl.pallas_call(lambda *refs: layer_kernel(n, *refs), out_shape=(shape((to...]
where the time goes in v4:
time: 72.6 us; the launch traced here: 71.7 us
  Pallas kernels  71.1 us (98%)
    pallas_call x1, Pallas kernels, by_heads(): pl.pallas_call(lambda *refs: layer_kernel(n, *refs), out_shape=(shape((to...  69.9 us

profile of v4, /device:TPU:11, one launch (start us, length us, event | category | flops | bytes accessed | tf_op | source)
XLA Modules:
  0.0 71.7 jit_solution(14328842682055728931)
XLA Ops:
  0.6 69.9 %layer.1 = (bf16[128,2048]{1,0:T(8,128)(2,1)S(1)}, bf16[128,1024]{1,0:T(8,128)(2,1)S(1)}, bf16[128,1024]{1,0:T(8,128)(2,1)S(1)}, bf16[128,1024]{1,0:T(8,128)(2,1)S(1)}, f32[32,2048]{1,0:T(8,128)S(1)}) custom-call(bf16[128,1024]{1,0:T(8,128)(2,1)} %bitcast.9, bf16[128,1024]{1,0:T(8,128)(2,1)} %bitcast.10, bf16[128,1024]{1,0:T(8,128)(2,1)} %bitcast.11, ...), custom_call_target="tpu_custom_call" | custom-call | tf_op jit(solution)/shard_map/layer/pallas_call | solution.py:792
  70.5 1.2 %deliver.1 = (bf16[128,2048]{1,0:T(8,128)(2,1)}, bf16[128,1024]{1,0:T(8,128)(2,1)}, bf16[128,1024]{1,0:T(8,128)(2,1)}, bf16[128,1024]{1,0:T(8,128)(2,1)}, f32[32,2048]{1,0:T(8,128)}) custom-call(bf16[128,2048]{1,0:T(8,128)(2,1)S(1)} %get-tuple-element.15.refs_0_, bf16[128,1024]{1,0:T(8,128)(2,1)S(1)} %get-tuple-element.16.refs_1_, ...), custom_call_target="tpu_custom_call" | custom-call | tf_op jit(solution)/shard_map/deliver/pallas_call | solution.py:835

commit v5 on v4

--- a/solution.py
+++ b/solution.py
@@ -547,14 +547,6 @@
     heads_wait(2, vh)
     vt[...] = vh[...].astype(f32).T.astype(bf16)
 
-    def attend(o, carry):
-        part = two_rows(o)
-        att_t = jnp.dot(vt[...], prob[:, part], preferred_element_type=f32)
-        att[part] = att_t.T.astype(bf16)
-        return carry
-
-    lax.fori_loop(0, n // 2, attend, 0)
-
     def att_copy(i):
         plane = lax.rem(zed + i, planes)
         return remote(
@@ -563,8 +555,16 @@
             {"cp": 2 * plane + why, "fsdp": 2 * ex + zed // 2},
         )
 
+    def attend(o, carry):
+        part = two_rows(o)
+        att_t = jnp.dot(vt[...], prob[:, part], preferred_element_type=f32)
+        att[part] = att_t.T.astype(bf16)
+        return carry
+
     for i in (2, 1, 3):
+        attend(lax.rem(zed + i, planes), 0)
         launch(att_copy(i))
+    attend(zed, 0)
 
     @pl.when(keeper)
     def _():
@@ -622,13 +622,22 @@
 
     seq_wait(ga_s, ga_r, lambda source: ga.at[two_rows(source)])
 
-    def value_step(o, carry):
-        part = two_rows(o)
+    def piece_send(t, source, target, plane):
+        for h in range(2):
+            i = lax.rem(2 * plane + h + n - me, n)
+
+            @pl.when(i > 0)
+            def _():
+                out_copy(t, i, source, target).start()
+
+    def value_step(b, carry):
+        plane = lax.rem(zed + 2 + b, planes)
+        part = two_rows(plane)
         dvh[part] = jnp.dot(prob[part], ga[...], preferred_element_type=f32).astype(bf16)
+        piece_send(2, dvh, dv, plane)
         return carry
 
-    lax.fori_loop(0, n // 2, value_step, 0)
-    out_send(2, dvh, dv)
+    lax.fori_loop(0, planes, value_step, 0)
     dv[:, head_cols(me)] = dvh[rows(me)]
 
     def backward(i, carry):
@@ -693,13 +702,14 @@
         def _():
             dw_send(j)
 
-    def key_step(o, carry):
-        part = two_rows(o)
+    def key_step(b, carry):
+        plane = lax.rem(zed + 2 + b, planes)
+        part = two_rows(plane)
         dkh[part] = jnp.dot(dsb[part], qh[...], preferred_element_type=f32).astype(bf16)
+        piece_send(1, dkh, dk, plane)
         return carry
 
-    lax.fori_loop(0, n // 2, key_step, 0)
-    out_send(1, dkh, dk)
+    lax.fori_loop(0, planes, key_step, 0)
     dk[:, head_cols(me)] = dkh[rows(me)]
 
     @pl.when(gateway)
@@ -731,6 +741,8 @@
         copy.wait_send()
     for i in offsets:
         out_copy(0, i, dqh, dq).wait_send()
+        out_copy(2, i, dvh, dv).wait_send()
+        out_copy(1, i, dkh, dk).wait_send()
 
     @pl.when(jnp.logical_not(root))
     def _():

time: 72.6 us -> 70.8 us (0.975)
  Pallas kernels: 71.1 us -> 69.1 us
    pallas_call x1, Pallas kernels: 69.9 us -> 67.9 us  [by_heads(): pl.pallas_call(lambda *refs: layer_kernel(n, *refs), out_shape=(shape((to...]
where the time goes in v5:
time: 70.8 us; the launch traced here: 69.7 us
  Pallas kernels  69.1 us (98%)
    pallas_call x1, Pallas kernels, by_heads(): pl.pallas_call(lambda *refs: layer_kernel(n, *refs), out_shape=(shape((to...  67.9 us

profile of v5, /device:TPU:11, one launch (start us, length us, event | category | flops | bytes accessed | tf_op | source)
XLA Modules:
  0.0 69.7 jit_solution(16041657345378412887)
XLA Ops:
  0.6 67.9 %layer.1 = (bf16[128,2048]{1,0:T(8,128)(2,1)S(1)}, bf16[128,1024]{1,0:T(8,128)(2,1)S(1)}, bf16[128,1024]{1,0:T(8,128)(2,1)S(1)}, bf16[128,1024]{1,0:T(8,128)(2,1)S(1)}, f32[32,2048]{1,0:T(8,128)S(1)}) custom-call(bf16[128,1024]{1,0:T(8,128)(2,1)} %bitcast.9, bf16[128,1024]{1,0:T(8,128)(2,1)} %bitcast.10, bf16[128,1024]{1,0:T(8,128)(2,1)} %bitcast.11, ...), custom_call_target="tpu_custom_call" | custom-call | tf_op jit(solution)/shard_map/layer/pallas_call | solution.py:804
  68.5 1.2 %deliver.1 = (bf16[128,2048]{1,0:T(8,128)(2,1)}, bf16[128,1024]{1,0:T(8,128)(2,1)}, bf16[128,1024]{1,0:T(8,128)(2,1)}, bf16[128,1024]{1,0:T(8,128)(2,1)}, f32[32,2048]{1,0:T(8,128)}) custom-call(bf16[128,2048]{1,0:T(8,128)(2,1)S(1)} %get-tuple-element.15.refs_0_, bf16[128,1024]{1,0:T(8,128)(2,1)S(1)} %get-tuple-element.16.refs_1_, ...), custom_call_target="tpu_custom_call" | custom-call | tf_op jit(solution)/shard_map/deliver/pallas_call | solution.py:847

commit v6 on v5

--- a/solution.py
+++ b/solution.py
@@ -314,7 +314,7 @@
                     device_id={"cp": lax.rem(me + i, n), "fsdp": lax.rem(col + j, cols)},
                     device_id_type=MESH,
                 )
-    for copy in loads:
+    for copy in loads[:3]:
         copy.wait()
     pl.semaphore_wait(barrier, n * cols - 1)
 
@@ -380,6 +380,8 @@
     launch(remote(up, mine_up, up_s.at[1], up_r.at[1], beside))
     heads_send(0, k, kh)
     launch(remote(up, mine_up, up_s.at[0], up_r.at[0], mate))
+    for copy in loads[3:]:
+        copy.wait()
     heads_send(1, q, qh)
 
     @pl.when(root)
@@ -443,11 +445,11 @@
             piece_poll(p)
 
     heads_wait(0, kh)
-    heads_send(2, v, vh)
     kt[...] = kh[...].astype(f32).T.astype(bf16)
     beside_up = ups.at[rows(2 * core + 1 - why)]
     remote(beside_up, beside_up, up_s.at[1], up_r.at[1], beside).wait_recv()
     launch(remote(beside_up, beside_up, up_s.at[2], up_r.at[2], mate))
+    heads_send(2, v, vh)
     @pl.when(far)
     def _():
         for p in range(cols // 2):

time: 70.8 us -> 70.7 us (level)
  no operation moved by 1% of the time
where the time goes in v6:
time: 70.7 us; the launch traced here: 69.8 us
  Pallas kernels  69.2 us (98%)
    pallas_call x1, Pallas kernels, by_heads(): pl.pallas_call(lambda *refs: layer_kernel(n, *refs), out_shape=(shape((to...  68 us

profile of v6, /device:TPU:11, one launch (start us, length us, event | category | flops | bytes accessed | tf_op | source)
XLA Modules:
  0.0 69.8 jit_solution(7899911644982306758)
XLA Ops:
  0.6 68.0 %layer.1 = (bf16[128,2048]{1,0:T(8,128)(2,1)S(1)}, bf16[128,1024]{1,0:T(8,128)(2,1)S(1)}, bf16[128,1024]{1,0:T(8,128)(2,1)S(1)}, bf16[128,1024]{1,0:T(8,128)(2,1)S(1)}, f32[32,2048]{1,0:T(8,128)S(1)}) custom-call(bf16[128,1024]{1,0:T(8,128)(2,1)} %bitcast.9, bf16[128,1024]{1,0:T(8,128)(2,1)} %bitcast.10, bf16[128,1024]{1,0:T(8,128)(2,1)} %bitcast.11, ...), custom_call_target="tpu_custom_call" | custom-call | tf_op jit(solution)/shard_map/layer/pallas_call | solution.py:806
  68.7 1.2 %deliver.1 = (bf16[128,2048]{1,0:T(8,128)(2,1)}, bf16[128,1024]{1,0:T(8,128)(2,1)}, bf16[128,1024]{1,0:T(8,128)(2,1)}, bf16[128,1024]{1,0:T(8,128)(2,1)}, f32[32,2048]{1,0:T(8,128)}) custom-call(bf16[128,2048]{1,0:T(8,128)(2,1)S(1)} %get-tuple-element.15.refs_0_, bf16[128,1024]{1,0:T(8,128)(2,1)S(1)} %get-tuple-element.16.refs_1_, ...), custom_call_target="tpu_custom_call" | custom-call | tf_op jit(solution)/shard_map/deliver/pallas_call | solution.py:849
